TPU v7x, 768 devices: a whole 4x8x12 slice. The times are simulated.
768 devices in a mesh: gx: 12 (over z), gy: 4 (over x), gz: 16 (over y, core).
Axes of the slice: x: 4, y: 8, z: 12, core: 2. Of those that a mesh axis runs over, the one named last changes fastest.
Arguments:
- old_slots: bfloat16 [12, 4, 256, 4096], P('gx', 'gy', 'gz'), may hold values from -6 to 6
- old_ids: int32 [12, 4, 256], P('gx', 'gy', 'gz'), may hold values from -1 to 127, as said below
- old_owner: int32 [12, 4, 128], P('gx', 'gy'), may hold values from 0 to 15, as said below
- coefficient: float32 [192, 64, 2048], P('gx', 'gy', 'gz'), may hold values from 0.2 to 5
Outputs:
- solution: float32 [192, 64, 2048], P('gx', 'gy', 'gz')
Inputs may be any that keep to these rules, and one draw needn't show every extreme that they name: old_owner[a, c, b] is the index along gz of the device that held box b of box column (a, c) before the move; no device holds more than 16 boxes of a column and some device holds exactly 16; no device holds more than 2 of the 8 boxes with one value of b // 8, and that bound is reached. old_ids[a, c, g * 16 + q] is the box held in slot q of device g of box column (a, c), or -1 for an empty slot; it agrees with old_owner and each box stands in exactly one slot.
All inputs are finite; a program needn't handle non-finite values.
Results may differ from a plain program's by a relative error of at most 0.0003.
Values may be sent and summed in bfloat16 or wider, within the bound.
A program may use at most 64 MiB of HBM per device.

v0:
```python
import jax
import jax.numpy as jnp
from jax import lax
from jax.sharding import Mesh
from jax.sharding import PartitionSpec as P

BOX = 16
NB = 8
SEND = 2
SWEEPS = 2
GX_GY_GZ = ("gx", "gy", "gz_0", "gz_1")
GZ = ("gz_0", "gz_1")


def with_halo(cells, sides, width):
    for axis, dim in sides:
        count = lax.axis_size(axis)
        ends = count - 1
        head = lax.slice_in_dim(cells, 0, width, axis=dim)
        tail = lax.slice_in_dim(cells, cells.shape[dim] - width, cells.shape[dim], axis=dim)
        cells = jnp.concatenate(
            [
                lax.ppermute(tail, axis, [(i, (i + 1) % count) for i in range(ends)]),
                cells,
                lax.ppermute(head, axis, [((i + 1) % count, i) for i in range(ends)]),
            ],
            axis=dim,
        )
    return cells


def one_axis_at_a_time(value, axes):
    for axis in axes:
        value = lax.psum(value, axis)
    return value


def rims(values, depth):
    return with_halo(values, (("gx", 0), ("gy", 1), (GZ, 2)), depth)


def inner(padded):
    return padded[1:-1, 1:-1, 1:-1]


def operator_parts(padded):
    face_first = 0.5 * (padded[:-1, 1:-1, 1:-1] + padded[1:, 1:-1, 1:-1])
    face_second = 0.5 * (padded[1:-1, :-1, 1:-1] + padded[1:-1, 1:, 1:-1])
    face_third = 0.5 * (padded[1:-1, 1:-1, :-1] + padded[1:-1, 1:-1, 1:])
    diagonal = (
        face_first[:-1]
        + face_first[1:]
        + face_second[:, :-1]
        + face_second[:, 1:]
        + face_third[:, :, :-1]
        + face_third[:, :, 1:]
    )
    return (face_first, face_second, face_third, diagonal)


def neighbours(padded, stencil):
    face_first, face_second, face_third, diagonal = stencil
    summed = face_first[:-1] * padded[:-2, 1:-1, 1:-1] + face_first[1:] * padded[2:, 1:-1, 1:-1]
    summed = (
        summed
        + face_second[:, :-1] * padded[1:-1, :-2, 1:-1]
        + face_second[:, 1:] * padded[1:-1, 2:, 1:-1]
    )
    summed = (
        summed
        + face_third[:, :, :-1] * padded[1:-1, 1:-1, :-2]
        + face_third[:, :, 1:] * padded[1:-1, 1:-1, 2:]
    )
    return summed


def red_cells(shape, margin):
    index_first = lax.broadcasted_iota(jnp.int32, shape, 0)
    index_second = lax.broadcasted_iota(jnp.int32, shape, 1)
    index_third = lax.broadcasted_iota(jnp.int32, shape, 2)
    return (index_first + index_second + index_third + margin) % 2 == 0


def relax(padded, source, stencil, factor, chosen):
    fresh = (factor * source + neighbours(padded, stencil)) / stencil[3]
    return jnp.where(chosen, fresh, inner(padded))


def apply_operator(values, stencil, factor):
    return (stencil[3] * values - neighbours(rims(values, 1), stencil)) / factor


def sweep_thin(values, source, stencil, factor, red_mask, starting):
    if starting:
        values = jnp.where(red_mask, factor * source / stencil[3], 0.0)
    else:
        values = relax(rims(values, 1), source, stencil, factor, red_mask)
    return relax(rims(values, 1), source, stencil, factor, jnp.logical_not(red_mask))


def smooth_thin(values, source, stencil, factor, starting):
    red_mask = red_cells(source.shape, 0)
    for counter in range(SWEEPS):
        values = sweep_thin(values, source, stencil, factor, red_mask, starting and counter == 0)
    return values


def sweep_deep(
    values, source_rim, stencil_rim, stencil_block, factor, red_rim, black_block, starting
):
    if starting:
        coloured = jnp.where(red_rim, factor * source_rim / stencil_rim[3], 0.0)
    else:
        coloured = relax(rims(values, 2), source_rim, stencil_rim, factor, red_rim)
    return relax(coloured, inner(source_rim), stencil_block, factor, black_block)


def coarsen(values):
    extent_first, extent_second, extent_third = values.shape
    grouped = values.reshape(extent_first // 2, 2, extent_second // 2, 2, extent_third // 2, 2)
    return grouped.mean(axis=(1, 3, 5))


def refine(values):
    return jnp.repeat(jnp.repeat(jnp.repeat(values, 2, axis=0), 2, axis=1), 2, axis=2)


def bottom_solve(rhs_low, stencil, factor):
    image_low = apply_operator(rhs_low, stencil, factor)
    second_image = apply_operator(image_low, stencil, factor)
    totals = (
        one_axis_at_a_time(jnp.sum(rhs_low * rhs_low), GX_GY_GZ),
        one_axis_at_a_time(jnp.sum(rhs_low * image_low), GX_GY_GZ),
        one_axis_at_a_time(jnp.sum(image_low * image_low), GX_GY_GZ),
        one_axis_at_a_time(jnp.sum(second_image * rhs_low), GX_GY_GZ),
        one_axis_at_a_time(jnp.sum(second_image * image_low), GX_GY_GZ),
        one_axis_at_a_time(jnp.sum(second_image * second_image), GX_GY_GZ),
    )
    norm_rhs, along_rhs, norm_image, second_rhs, second_along, norm_second = totals
    alpha_step = norm_rhs / along_rhs
    turned_rest = (
        along_rhs
        - alpha_step * norm_image
        - alpha_step * second_rhs
        + alpha_step * alpha_step * second_along
    )
    turned_norm = (
        norm_image - 2.0 * alpha_step * second_along + alpha_step * alpha_step * norm_second
    )
    rest_low = rhs_low - alpha_step * image_low
    omega_step = turned_rest / turned_norm
    return alpha_step * rhs_low + omega_step * rest_low


def widen(items):
    return items.astype(jnp.float32)


def move_boxes(old_slots, old_ids, old_owner):
    slot_rows = old_slots.reshape(old_slots.shape[2], old_slots.shape[3])
    slot_ids = old_ids.reshape(-1)
    owner_map = old_owner.reshape(-1)
    groups = lax.axis_size(GZ)
    my_index = lax.axis_index(GZ)
    capacity = slot_ids.shape[0]
    filled = slot_ids >= 0
    target = jnp.where(filled, slot_ids // NB, -1)
    earlier = (
        (target[None, :] == target[:, None])
        & (slot_ids[None, :] < slot_ids[:, None])
        & filled[None, :]
    )
    ranking = jnp.sum(earlier.astype(jnp.int32), axis=1)
    send_row = jnp.where(filled, target * SEND + ranking, -1)
    picker = lax.broadcasted_iota(jnp.int32, (groups * SEND, capacity), 0) == send_row[None, :]
    outgoing = jnp.dot(
        picker.astype(jnp.bfloat16), slot_rows, preferred_element_type=jnp.float32
    ).astype(jnp.bfloat16)
    ranked = outgoing.reshape(groups, SEND, outgoing.shape[1])
    incoming = widen(lax.all_to_all(ranked, GZ, split_axis=0, concat_axis=0, tiled=True)).reshape(
        groups * SEND, outgoing.shape[1]
    )
    arriving = lax.dynamic_slice_in_dim(owner_map, my_index * NB, NB)
    later_index = lax.broadcasted_iota(jnp.int32, (NB, NB), 0)
    before = (arriving[None, :] == arriving[:, None]) & (
        lax.broadcasted_iota(jnp.int32, (NB, NB), 1) < later_index
    )
    order_within = jnp.sum(before.astype(jnp.int32), axis=1)
    chosen_boxes = jnp.take(incoming, arriving * SEND + order_within, axis=0)
    stacked = chosen_boxes.reshape(NB, BOX, BOX, BOX).transpose(1, 2, 0, 3)
    return stacked.reshape(BOX, BOX, NB * BOX)


def per_device(old_slots, old_ids, old_owner, coefficient):
    source_fine = move_boxes(old_slots, old_ids, old_owner)
    coefficient_rim = rims(coefficient, 2)
    inside = inner(coefficient_rim) > 0.0
    face_first, face_second, face_third, diagonal = operator_parts(coefficient_rim)
    stencil_rim = (face_first, face_second, face_third, jnp.where(inside, diagonal, 1.0))
    stencil_fine = (inner(face_first), inner(face_second), inner(face_third), inner(diagonal))
    source_rim = rims(source_fine, 1)
    red_rim = jnp.logical_and(red_cells(inside.shape, 1), inside)
    black_fine = jnp.logical_not(red_cells(source_fine.shape, 0))

    def smooth_fine(values, starting):
        for counter in range(SWEEPS):
            values = sweep_deep(
                values,
                source_rim,
                stencil_rim,
                stencil_fine,
                1.0,
                red_rim,
                black_fine,
                starting and counter == 0,
            )
        return values

    fine_values = smooth_fine(jnp.zeros_like(source_fine), True)
    residual_fine = source_fine - apply_operator(fine_values, stencil_fine, 1.0)
    coefficient_mid = coarsen(coefficient)
    stencil_mid = operator_parts(rims(coefficient_mid, 1))
    source_mid = coarsen(residual_fine)
    middle_values = smooth_thin(jnp.zeros_like(source_mid), source_mid, stencil_mid, 4.0, True)
    residual_mid = source_mid - apply_operator(middle_values, stencil_mid, 4.0)
    coefficient_low = coarsen(coefficient_mid)
    stencil_low = operator_parts(rims(coefficient_low, 1))
    bottom_values = bottom_solve(coarsen(residual_mid), stencil_low, 16.0)
    middle_values = smooth_thin(
        middle_values + refine(bottom_values), source_mid, stencil_mid, 4.0, False
    )
    return smooth_fine(fine_values + refine(middle_values), False)


def solution(mesh):
    split = Mesh(
        mesh.devices.reshape(mesh.shape["gx"], mesh.shape["gy"], 8, 2), ("gx", "gy", "gz_0", "gz_1")
    )
    placed = (P("gx", "gy", GZ, None), P("gx", "gy", GZ), P("gx", "gy", None), P("gx", "gy", GZ))
    return jax.shard_map(
        per_device, mesh=split, in_specs=placed, out_specs=P("gx", "gy", GZ), check_vma=False
    )
```

profile of v0, /device:TPU:1, one launch (start us, length us, event | category | flops | bytes accessed | tf_op | source)
XLA Modules:
  0.0 586.5 jit_solution(17053579178227308648)
XLA Ops:
  2.1 5.4 collective-permute-start
  11.5 12.9 %all-to-all-start = ((bf16[16,2,4096]{2,1,0:T(2,128)(2,1)}), bf16[16,2,4096]{2,1,0:T(2,128)(2,1)S(1)}, u32[]{:S(2)}, u32[]{:S(2)}) async-start(bf16[16,2,4096]{2,1,0:T(2,128)(2,1)} %reshape.187), calls=%async_computation | async-start | bytes 524288 | tf_op jit(solution)/shard_map/all_to_all | solution.py:180
  24.5 10.6 %reshape.192 = f32[8,2,8,2,64,2]{5,4,3,2,1,0:T(8,128)} reshape(f32[16,16,128]{2,1,0:T(8,128)} %param.7) | data formatting | bytes 262144 | tf_op jit(solution)/shard_map/reshape | solution.py:120
  35.0 4.0 reduce_sum.114
  48.5 5.0 collective-permute-start.4
  56.6 4.4 collective-permute-done.5
  65.4 4.3 collective-permute-start.6
  71.7 4.9 collective-permute-done.7
  84.3 4.3 collective-permute-start.10
  91.5 4.4 collective-permute-done.11
  97.1 4.0 collective-permute-start.12
  115.4 4.0 collective-permute-start.16
  122.5 4.4 collective-permute-done.17
  129.2 5.5 collective-permute-start.18
  147.3 4.2 collective-permute-start.22
  154.4 4.4 collective-permute-done.23
  159.2 9.8 %reshape.191 = f32[8,2,8,2,64,2]{5,4,3,2,1,0:T(8,128)} reshape(f32[16,16,128]{2,1,0:T(8,128)S(1)} %fusion.55) | data formatting | bytes 262144 | tf_op jit(solution)/shard_map/reshape | solution.py:120
  169.0 4.0 reduce_sum.113
  173.1 5.5 collective-permute-start.30
  189.4 4.3 collective-permute-start.34
  195.7 3.8 collective-permute-done.35
  199.6 4.1 collective-permute-start.36
  205.0 4.5 collective-permute-done.37
  215.7 4.5 collective-permute-start.40
  222.1 3.8 collective-permute-done.41
  226.7 4.8 collective-permute-start.42
  244.2 5.6 collective-permute-start.46
  258.0 4.0 collective-permute-start.48
  266.3 4.0 collective-permute-start.50
  274.8 6.5 %collective-permute-start.52 = (f32[10,10,1]{2,1,0:T(8,128)S(1)}, f32[10,10,1]{2,1,0:T(8,128)S(1)}, u32[]{:S(2)}, u32[]{:S(2)}) collective-permute-start(f32[10,10,1]{2,1,0:T(8,128)S(1)} %get-tuple-element.84), channel_id=1, source_target_pairs={{0,1},{1,2},{2,3},{3,4},{4,5},{5,6},{6,7},{7,8},{8,9},{9,10},{10,1... | collective-permute-start | bytes 1208 | tf_op jit(solution)/shard_map/ppermute | solution.py:23
  291.1 4.3 collective-permute-start.60
  309.2 6.1 %collective-permute-start.64 = (f32[6,6,1]{2,1,0:T(8,128)S(1)}, f32[6,6,1]{2,1,0:T(8,128)S(1)}, u32[]{:S(2)}, u32[]{:S(2)}) collective-permute-start(f32[6,6,1]{2,1,0:T(8,128)S(1)} %get-tuple-element.134), channel_id=1, source_target_pairs={{0,1},{1,2},{2,3},{3,4},{4,5},{5,6},{6,7},{7,8},{8,9},{9,10},{10,1... | collective-permute-start | bytes 440 | tf_op jit(solution)/shard_map/ppermute | solution.py:23
  321.4 4.0 collective-permute-start.66
  336.4 6.3 %collective-permute-start.70 = (f32[6,6,1]{2,1,0:T(8,128)S(1)}, f32[6,6,1]{2,1,0:T(8,128)S(1)}, u32[]{:S(2)}, u32[]{:S(2)}) collective-permute-start(f32[6,6,1]{2,1,0:T(8,128)S(1)} %get-tuple-element.130), channel_id=1, source_target_pairs={{0,1},{1,2},{2,3},{3,4},{4,5},{5,6},{6,7},{7,8},{8,9},{9,10},{10,1... | collective-permute-start | bytes 440 | tf_op jit(solution)/shard_map/ppermute | solution.py:23
  349.5 23.8 %all-reduce = (f32[]{:T(128)}, f32[]{:T(128)}, f32[]{:T(128)}, f32[]{:T(128)}, f32[]{:T(128)}, /*index=5*/f32[]{:T(128)}) all-reduce(f32[]{:T(128)} %get-tuple-element.9, f32[]{:T(128)} %get-tuple-element.7, f32[]{:T(128)} %get-tuple-element.10, f32[]{:T(128)} %get-tuple-element.8, ...), channel_id=1, replica_groups=mesh['gx'=12,'gy'=4,'gz_0'=8,'gz_1'=2] {'gx'}, use_global_device_ids=true, to_apply=%region_6.7 | all-reduce | flops 6 | bytes 48 | tf_op jit(solution)/shard_map/psum | solution.py:34
  373.3 6.7 %all-reduce.2 = (f32[]{:T(128)}, f32[]{:T(128)}, f32[]{:T(128)}, f32[]{:T(128)}, f32[]{:T(128)}, /*index=5*/f32[]{:T(128)}) all-reduce(f32[]{:T(128)} %get-tuple-element.11, f32[]{:T(128)} %get-tuple-element.12, f32[]{:T(128)} %get-tuple-element.13, f32[]{:T(128)} %get-tuple-element.14, ...), channel_id=1, replica_groups=mesh['gx'=12,'gy'=4,'gz_0'=8,'gz_1'=2] {'gy'}, use_global_device_ids=true, to_apply=%region_7.8 | all-reduce | flops 6 | bytes 48 | tf_op jit(solution)/shard_map/psum | solution.py:34
  380.0 21.9 %all-reduce.1 = (f32[]{:T(128)}, f32[]{:T(128)}, f32[]{:T(128)}, f32[]{:T(128)}, f32[]{:T(128)}, /*index=5*/f32[]{:T(128)}) all-reduce(f32[]{:T(128)} %get-tuple-element.23, f32[]{:T(128)} %get-tuple-element.24, f32[]{:T(128)} %get-tuple-element.25, f32[]{:T(128)} %get-tuple-element.26, ...), channel_id=1, replica_groups=mesh['gx'=12,'gy'=4,'gz_0'=8,'gz_1'=2] {'gz_0'}, use_global_device_ids=true, to_apply=%region_8.9 | all-reduce | flops 6 | bytes 48 | tf_op jit(solution)/shard_map/psum | solution.py:34
  402.0 10.1 %all-reduce.3 = (f32[]{:T(128)}, f32[]{:T(128)}, f32[]{:T(128)}, f32[]{:T(128)}, f32[]{:T(128)}, /*index=5*/f32[]{:T(128)}) all-reduce(f32[]{:T(128)} %get-tuple-element.17, f32[]{:T(128)} %get-tuple-element.18, f32[]{:T(128)} %get-tuple-element.19, ...), channel_id=1, replica_groups=mesh['gx'=12,'gy'=4,'gz_0'=8,'gz_1'=2] {'gz_1'}, use_global_device_ids=true, to_apply=%region_9.10 | all-reduce | flops 6 | bytes 48 | tf_op jit(solution)/shard_map/psum | solution.py:34
  433.4 6.5 %collective-permute-start.76 = (f32[10,10,1]{2,1,0:T(8,128)S(1)}, f32[10,10,1]{2,1,0:T(8,128)S(1)}, u32[]{:S(2)}, u32[]{:S(2)}) collective-permute-start(f32[10,10,1]{2,1,0:T(8,128)S(1)} %get-tuple-element.82), channel_id=1, source_target_pairs={{0,1},{1,2},{2,3},{3,4},{4,5},{5,6},{6,7},{7,8},{8,9},{9,10},{10,1... | collective-permute-start | bytes 1208 | tf_op jit(solution)/shard_map/ppermute | solution.py:23
  441.8 3.8 collective-permute-done.77
  460.6 4.4 collective-permute-start.82
  471.0 4.8 collective-permute-start.84
  488.0 4.4 collective-permute-start.88
  512.5 4.7 collective-permute-start.94
  541.1 4.8 collective-permute-start.100
  549.0 4.4 collective-permute-done.101
  570.6 4.4 collective-permute-start.106
  578.2 4.4 collective-permute-done.107
  (367 shorter events, 292.9 us)
Async XLA Ops:
  0.8 41.7 %collective-permute-start.1 = (f32[2,16,128]{2,1,0:T(8,128)S(1)}, f32[2,16,128]{2,1,0:T(8,128)S(1)}, u32[]{:S(2)}, u32[]{:S(2)}) collective-permute-start(f32[2,16,128]{2,1,0:T(8,128)S(1)} %get-tuple-element.74), channel_id=1, source_target_pairs={{64,0},{128,64},{192,128},{256,192},{320,256},{384,320},{448,384},... | collective-permute-start | bytes 49160 | tf_op jit(solution)/shard_map/ppermute | solution.py:25
  2.1 40.3 %collective-permute-start = (f32[2,16,128]{2,1,0:T(8,128)S(1)}, f32[2,16,128]{2,1,0:T(8,128)S(1)}, u32[]{:S(2)}, u32[]{:S(2)}) collective-permute-start(f32[2,16,128]{2,1,0:T(8,128)S(1)} %get-tuple-element.75), channel_id=1, source_target_pairs={{0,64},{64,128},{128,192},{192,256},{256,320},{320,384},{384,448},... | collective-permute-start | bytes 49160 | tf_op jit(solution)/shard_map/ppermute | solution.py:23
  11.5 49.8 %all-to-all-start = ((bf16[16,2,4096]{2,1,0:T(2,128)(2,1)}), bf16[16,2,4096]{2,1,0:T(2,128)(2,1)S(1)}, u32[]{:S(2)}, u32[]{:S(2)}) async-start(bf16[16,2,4096]{2,1,0:T(2,128)(2,1)} %reshape.187), calls=%async_computation | async-start | bytes 524288 | tf_op jit(solution)/shard_map/all_to_all | solution.py:180
  39.1 63.3 %collective-permute-start.24 = (f32[1,8,64]{2,1,0:T(8,128)S(1)}, f32[1,8,64]{2,1,0:T(8,128)S(1)}, u32[]{:S(2)}, u32[]{:S(2)}) collective-permute-start(f32[1,8,64]{2,1,0:T(8,128)S(1)} %get-tuple-element.128), channel_id=1, source_target_pairs={{0,64},{64,128},{128,192},{192,256},{256,320},{320,384},{384,448},... | collective-permute-start | bytes 6152 | tf_op jit(solution)/shard_map/ppermute | solution.py:23
  40.7 61.7 %collective-permute-start.25 = (f32[1,8,64]{2,1,0:T(8,128)S(1)}, f32[1,8,64]{2,1,0:T(8,128)S(1)}, u32[]{:S(2)}, u32[]{:S(2)}) collective-permute-start(f32[1,8,64]{2,1,0:T(8,128)S(1)} %get-tuple-element.129), channel_id=1, source_target_pairs={{64,0},{128,64},{192,128},{256,192},{320,256},{384,320},{448,384},... | collective-permute-start | bytes 6152 | tf_op jit(solution)/shard_map/ppermute | solution.py:25
  48.5 8.1 %collective-permute-start.4 = (f32[20,20,2]{2,1,0:T(8,128)S(1)}, f32[20,20,2]{2,1,0:T(8,128)S(1)}, u32[]{:S(2)}, u32[]{:S(2)}) collective-permute-start(f32[20,20,2]{2,1,0:T(8,128)S(1)} %get-tuple-element.48), channel_id=1, source_target_pairs={{0,1},{1,2},{2,3},{3,4},{4,5},{5,6},{6,7},{7,8},{8,9},{9,10},{10,1... | collective-permute-start | bytes 9608 | tf_op jit(solution)/shard_map/ppermute | solution.py:23
  53.5 7.5 %collective-permute-start.5 = (f32[20,20,2]{2,1,0:T(8,128)S(1)}, f32[20,20,2]{2,1,0:T(8,128)S(1)}, u32[]{:S(2)}, u32[]{:S(2)}) collective-permute-start(f32[20,20,2]{2,1,0:T(8,128)S(1)} %get-tuple-element.49), channel_id=1, source_target_pairs={{1,0},{2,1},{3,2},{4,3},{5,4},{6,5},{7,6},{8,7},{9,8},{10,9},{11,1... | collective-permute-start | bytes 9608 | tf_op jit(solution)/shard_map/ppermute | solution.py:25
  65.4 6.3 %collective-permute-start.6 = (f32[1,16,128]{2,1,0:T(8,128)S(1)}, f32[1,16,128]{2,1,0:T(8,128)S(1)}, u32[]{:S(2)}, u32[]{:S(2)}) collective-permute-start(f32[1,16,128]{2,1,0:T(8,128)S(1)} %slice.1002), channel_id=1, source_target_pairs={{0,64},{64,128},{128,192},{192,256},{256,320},{320,384},{384,448},... | collective-permute-start | bytes 24584 | tf_op jit(solution)/shard_map/ppermute | solution.py:23
  70.3 6.2 %collective-permute-start.7 = (f32[1,16,128]{2,1,0:T(8,128)S(1)}, f32[1,16,128]{2,1,0:T(8,128)S(1)}, u32[]{:S(2)}, u32[]{:S(2)}) collective-permute-start(f32[1,16,128]{2,1,0:T(8,128)S(1)} %slice.1004), channel_id=1, source_target_pairs={{64,0},{128,64},{192,128},{256,192},{320,256},{384,320},{448,384},... | collective-permute-start | bytes 24584 | tf_op jit(solution)/shard_map/ppermute | solution.py:25
  84.3 7.2 %collective-permute-start.10 = (f32[18,18,1]{2,1,0:T(8,128)S(1)}, f32[18,18,1]{2,1,0:T(8,128)S(1)}, u32[]{:S(2)}, u32[]{:S(2)}) collective-permute-start(f32[18,18,1]{2,1,0:T(8,128)S(1)} %get-tuple-element.52), channel_id=1, source_target_pairs={{0,1},{1,2},{2,3},{3,4},{4,5},{5,6},{6,7},{7,8},{8,9},{9,10},{10,1... | collective-permute-start | bytes 3896 | tf_op jit(solution)/shard_map/ppermute | solution.py:23
  88.6 7.3 %collective-permute-start.11 = (f32[18,18,1]{2,1,0:T(8,128)S(1)}, f32[18,18,1]{2,1,0:T(8,128)S(1)}, u32[]{:S(2)}, u32[]{:S(2)}) collective-permute-start(f32[18,18,1]{2,1,0:T(8,128)S(1)} %get-tuple-element.53), channel_id=1, source_target_pairs={{1,0},{2,1},{3,2},{4,3},{5,4},{6,5},{7,6},{8,7},{9,8},{10,9},{11,1... | collective-permute-start | bytes 3896 | tf_op jit(solution)/shard_map/ppermute | solution.py:25
  97.1 9.5 %collective-permute-start.12 = (f32[2,16,128]{2,1,0:T(8,128)S(1)}, f32[2,16,128]{2,1,0:T(8,128)S(1)}, u32[]{:S(2)}, u32[]{:S(2)}) collective-permute-start(f32[2,16,128]{2,1,0:T(8,128)S(1)} %get-tuple-element.72), channel_id=1, source_target_pairs={{0,64},{64,128},{128,192},{192,256},{256,320},{320,384},{384,448},... | collective-permute-start | bytes 49160 | tf_op jit(solution)/shard_map/ppermute | solution.py:23
  102.5 18.8 %collective-permute-start.26 = (f32[10,1,64]{2,1,0:T(1,128)S(1)}, f32[10,1,64]{2,1,0:T(1,128)S(1)}, u32[]{:S(2)}, u32[]{:S(2)}) collective-permute-start(f32[10,1,64]{2,1,0:T(1,128)S(1)} %get-tuple-element.110), channel_id=1, source_target_pairs={{0,16},{16,32},{32,48},{1,17},{17,33},{33,49},{2,18},{18,34},{34,5... | collective-permute-start | bytes 7688 | tf_op jit(solution)/shard_map/ppermute | solution.py:23
  105.3 16.0 %collective-permute-start.27 = (f32[10,1,64]{2,1,0:T(1,128)S(1)}, f32[10,1,64]{2,1,0:T(1,128)S(1)}, u32[]{:S(2)}, u32[]{:S(2)}) collective-permute-start(f32[10,1,64]{2,1,0:T(1,128)S(1)} %get-tuple-element.111), channel_id=1, source_target_pairs={{16,0},{32,16},{48,32},{17,1},{33,17},{49,33},{18,2},{34,18},{50,3... | collective-permute-start | bytes 7688 | tf_op jit(solution)/shard_map/ppermute | solution.py:25
  115.4 7.1 %collective-permute-start.16 = (f32[20,20,2]{2,1,0:T(8,128)S(1)}, f32[20,20,2]{2,1,0:T(8,128)S(1)}, u32[]{:S(2)}, u32[]{:S(2)}) collective-permute-start(f32[20,20,2]{2,1,0:T(8,128)S(1)} %get-tuple-element.46), channel_id=1, source_target_pairs={{0,1},{1,2},{2,3},{3,4},{4,5},{5,6},{6,7},{7,8},{8,9},{9,10},{10,1... | collective-permute-start | bytes 9608 | tf_op jit(solution)/shard_map/ppermute | solution.py:23
  119.4 7.5 %collective-permute-start.17 = (f32[20,20,2]{2,1,0:T(8,128)S(1)}, f32[20,20,2]{2,1,0:T(8,128)S(1)}, u32[]{:S(2)}, u32[]{:S(2)}) collective-permute-start(f32[20,20,2]{2,1,0:T(8,128)S(1)} %get-tuple-element.47), channel_id=1, source_target_pairs={{1,0},{2,1},{3,2},{4,3},{5,4},{6,5},{7,6},{8,7},{9,8},{10,9},{11,1... | collective-permute-start | bytes 9608 | tf_op jit(solution)/shard_map/ppermute | solution.py:25
  129.2 11.2 %collective-permute-start.18 = (f32[1,16,128]{2,1,0:T(8,128)S(1)}, f32[1,16,128]{2,1,0:T(8,128)S(1)}, u32[]{:S(2)}, u32[]{:S(2)}) collective-permute-start(f32[1,16,128]{2,1,0:T(8,128)S(1)} %get-tuple-element.70), channel_id=1, source_target_pairs={{0,64},{64,128},{128,192},{192,256},{256,320},{320,384},{384,448},... | collective-permute-start | bytes 24584 | tf_op jit(solution)/shard_map/ppermute | solution.py:23
  136.0 17.6 %collective-permute-start.28 = (f32[10,10,1]{2,1,0:T(8,128)S(1)}, f32[10,10,1]{2,1,0:T(8,128)S(1)}, u32[]{:S(2)}, u32[]{:S(2)}) collective-permute-start(f32[10,10,1]{2,1,0:T(8,128)S(1)} %get-tuple-element.92), channel_id=1, source_target_pairs={{0,1},{1,2},{2,3},{3,4},{4,5},{5,6},{6,7},{7,8},{8,9},{9,10},{10,1... | collective-permute-start | bytes 1208 | tf_op jit(solution)/shard_map/ppermute | solution.py:23
  138.1 15.5 %collective-permute-start.29 = (f32[10,10,1]{2,1,0:T(8,128)S(1)}, f32[10,10,1]{2,1,0:T(8,128)S(1)}, u32[]{:S(2)}, u32[]{:S(2)}) collective-permute-start(f32[10,10,1]{2,1,0:T(8,128)S(1)} %get-tuple-element.93), channel_id=1, source_target_pairs={{1,0},{2,1},{3,2},{4,3},{5,4},{6,5},{7,6},{8,7},{9,8},{10,9},{11,1... | collective-permute-start | bytes 1208 | tf_op jit(solution)/shard_map/ppermute | solution.py:25
  147.3 7.1 %collective-permute-start.22 = (f32[18,18,1]{2,1,0:T(8,128)S(1)}, f32[18,18,1]{2,1,0:T(8,128)S(1)}, u32[]{:S(2)}, u32[]{:S(2)}) collective-permute-start(f32[18,18,1]{2,1,0:T(8,128)S(1)} %get-tuple-element.50), channel_id=1, source_target_pairs={{0,1},{1,2},{2,3},{3,4},{4,5},{5,6},{6,7},{7,8},{8,9},{9,10},{10,1... | collective-permute-start | bytes 3896 | tf_op jit(solution)/shard_map/ppermute | solution.py:23
  151.5 7.3 %collective-permute-start.23 = (f32[18,18,1]{2,1,0:T(8,128)S(1)}, f32[18,18,1]{2,1,0:T(8,128)S(1)}, u32[]{:S(2)}, u32[]{:S(2)}) collective-permute-start(f32[18,18,1]{2,1,0:T(8,128)S(1)} %get-tuple-element.51), channel_id=1, source_target_pairs={{1,0},{2,1},{3,2},{4,3},{5,4},{6,5},{7,6},{8,7},{9,8},{10,9},{11,1... | collective-permute-start | bytes 3896 | tf_op jit(solution)/shard_map/ppermute | solution.py:25
  173.1 6.8 %collective-permute-start.30 = (f32[1,8,64]{2,1,0:T(8,128)S(1)}, f32[1,8,64]{2,1,0:T(8,128)S(1)}, u32[]{:S(2)}, u32[]{:S(2)}) collective-permute-start(f32[1,8,64]{2,1,0:T(8,128)S(1)} %get-tuple-element.126), channel_id=1, source_target_pairs={{0,64},{64,128},{128,192},{192,256},{256,320},{320,384},{384,448},... | collective-permute-start | bytes 6152 | tf_op jit(solution)/shard_map/ppermute | solution.py:23
  189.4 6.3 %collective-permute-start.34 = (f32[10,10,1]{2,1,0:T(8,128)S(1)}, f32[10,10,1]{2,1,0:T(8,128)S(1)}, u32[]{:S(2)}, u32[]{:S(2)}) collective-permute-start(f32[10,10,1]{2,1,0:T(8,128)S(1)} %get-tuple-element.90), channel_id=1, source_target_pairs={{0,1},{1,2},{2,3},{3,4},{4,5},{5,6},{6,7},{7,8},{8,9},{9,10},{10,1... | collective-permute-start | bytes 1208 | tf_op jit(solution)/shard_map/ppermute | solution.py:23
  215.7 6.4 %collective-permute-start.40 = (f32[10,10,1]{2,1,0:T(8,128)S(1)}, f32[10,10,1]{2,1,0:T(8,128)S(1)}, u32[]{:S(2)}, u32[]{:S(2)}) collective-permute-start(f32[10,10,1]{2,1,0:T(8,128)S(1)} %get-tuple-element.88), channel_id=1, source_target_pairs={{0,1},{1,2},{2,3},{3,4},{4,5},{5,6},{6,7},{7,8},{8,9},{9,10},{10,1... | collective-permute-start | bytes 1208 | tf_op jit(solution)/shard_map/ppermute | solution.py:23
  226.7 8.7 %collective-permute-start.42 = (f32[1,8,64]{2,1,0:T(8,128)}, f32[1,8,64]{2,1,0:T(8,128)S(1)}, u32[]{:S(2)}, u32[]{:S(2)}) collective-permute-start(f32[1,8,64]{2,1,0:T(8,128)} %get-tuple-element.122), channel_id=1, source_target_pairs={{0,64},{64,128},{128,192},{192,256},{256,320},{320,384},{384,448},... | collective-permute-start | bytes 6152 | tf_op jit(solution)/shard_map/ppermute | solution.py:23
  244.2 12.5 %collective-permute-start.46 = (f32[10,10,1]{2,1,0:T(8,128)S(1)}, f32[10,10,1]{2,1,0:T(8,128)S(1)}, u32[]{:S(2)}, u32[]{:S(2)}) collective-permute-start(f32[10,10,1]{2,1,0:T(8,128)S(1)} %get-tuple-element.86), channel_id=1, source_target_pairs={{0,1},{1,2},{2,3},{3,4},{4,5},{5,6},{6,7},{7,8},{8,9},{9,10},{10,1... | collective-permute-start | bytes 1208 | tf_op jit(solution)/shard_map/ppermute | solution.py:23
  249.9 6.9 %collective-permute-start.47 = (f32[10,10,1]{2,1,0:T(8,128)S(1)}, f32[10,10,1]{2,1,0:T(8,128)S(1)}, u32[]{:S(2)}, u32[]{:S(2)}) collective-permute-start(f32[10,10,1]{2,1,0:T(8,128)S(1)} %get-tuple-element.87), channel_id=1, source_target_pairs={{1,0},{2,1},{3,2},{4,3},{5,4},{6,5},{7,6},{8,7},{9,8},{10,9},{11,1... | collective-permute-start | bytes 1208 | tf_op jit(solution)/shard_map/ppermute | solution.py:25
  251.8 11.5 %collective-permute-start.54 = (f32[1,4,32]{2,1,0:T(4,128)S(1)}, f32[1,4,32]{2,1,0:T(4,128)S(1)}, u32[]{:S(2)}, u32[]{:S(2)}) collective-permute-start(f32[1,4,32]{2,1,0:T(4,128)S(1)} %get-tuple-element.144), channel_id=1, source_target_pairs={{0,64},{64,128},{128,192},{192,256},{256,320},{320,384},{384,448},... | collective-permute-start | bytes 1544 | tf_op jit(solution)/shard_map/ppermute | solution.py:23
  255.5 7.8 %collective-permute-start.55 = (f32[1,4,32]{2,1,0:T(4,128)S(1)}, f32[1,4,32]{2,1,0:T(4,128)S(1)}, u32[]{:S(2)}, u32[]{:S(2)}) collective-permute-start(f32[1,4,32]{2,1,0:T(4,128)S(1)} %get-tuple-element.145), channel_id=1, source_target_pairs={{64,0},{128,64},{192,128},{256,192},{320,256},{384,320},{448,384},... | collective-permute-start | bytes 1544 | tf_op jit(solution)/shard_map/ppermute | solution.py:25
  258.0 8.3 %collective-permute-start.48 = (f32[1,8,64]{2,1,0:T(8,128)S(1)}, f32[1,8,64]{2,1,0:T(8,128)S(1)}, u32[]{:S(2)}, u32[]{:S(2)}) collective-permute-start(f32[1,8,64]{2,1,0:T(8,128)S(1)} %get-tuple-element.120), channel_id=1, source_target_pairs={{0,64},{64,128},{128,192},{192,256},{256,320},{320,384},{384,448},... | collective-permute-start | bytes 6152 | tf_op jit(solution)/shard_map/ppermute | solution.py:23
  263.3 19.9 %collective-permute-start.56 = (f32[6,1,32]{2,1,0:T(1,128)S(1)}, f32[6,1,32]{2,1,0:T(1,128)S(1)}, u32[]{:S(2)}, u32[]{:S(2)}) collective-permute-start(f32[6,1,32]{2,1,0:T(1,128)S(1)} %get-tuple-element.138), channel_id=1, source_target_pairs={{0,16},{16,32},{32,48},{1,17},{17,33},{33,49},{2,18},{18,34},{34,5... | collective-permute-start | bytes 2312 | tf_op jit(solution)/shard_map/ppermute | solution.py:23
  265.0 18.2 %collective-permute-start.57 = (f32[6,1,32]{2,1,0:T(1,128)S(1)}, f32[6,1,32]{2,1,0:T(1,128)S(1)}, u32[]{:S(2)}, u32[]{:S(2)}) collective-permute-start(f32[6,1,32]{2,1,0:T(1,128)S(1)} %get-tuple-element.139), channel_id=1, source_target_pairs={{16,0},{32,16},{48,32},{17,1},{33,17},{49,33},{18,2},{34,18},{50,3... | collective-permute-start | bytes 2312 | tf_op jit(solution)/shard_map/ppermute | solution.py:25
  274.8 9.1 %collective-permute-start.52 = (f32[10,10,1]{2,1,0:T(8,128)S(1)}, f32[10,10,1]{2,1,0:T(8,128)S(1)}, u32[]{:S(2)}, u32[]{:S(2)}) collective-permute-start(f32[10,10,1]{2,1,0:T(8,128)S(1)} %get-tuple-element.84), channel_id=1, source_target_pairs={{0,1},{1,2},{2,3},{3,4},{4,5},{5,6},{6,7},{7,8},{8,9},{9,10},{10,1... | collective-permute-start | bytes 1208 | tf_op jit(solution)/shard_map/ppermute | solution.py:23
  291.1 12.0 %collective-permute-start.60 = (f32[1,4,32]{2,1,0:T(4,128)S(1)}, f32[1,4,32]{2,1,0:T(4,128)S(1)}, u32[]{:S(2)}, u32[]{:S(2)}) collective-permute-start(f32[1,4,32]{2,1,0:T(4,128)S(1)} %get-tuple-element.146), channel_id=1, source_target_pairs={{0,64},{64,128},{128,192},{192,256},{256,320},{320,384},{384,448},... | collective-permute-start | bytes 1544 | tf_op jit(solution)/shard_map/ppermute | solution.py:23
  295.3 7.8 %collective-permute-start.61 = (f32[1,4,32]{2,1,0:T(4,128)S(1)}, f32[1,4,32]{2,1,0:T(4,128)S(1)}, u32[]{:S(2)}, u32[]{:S(2)}) collective-permute-start(f32[1,4,32]{2,1,0:T(4,128)S(1)} %get-tuple-element.147), channel_id=1, source_target_pairs={{64,0},{128,64},{192,128},{256,192},{320,256},{384,320},{448,384},... | collective-permute-start | bytes 1544 | tf_op jit(solution)/shard_map/ppermute | solution.py:25
  297.5 19.8 %collective-permute-start.58 = (f32[6,6,1]{2,1,0:T(8,128)S(1)}, f32[6,6,1]{2,1,0:T(8,128)S(1)}, u32[]{:S(2)}, u32[]{:S(2)}) collective-permute-start(f32[6,6,1]{2,1,0:T(8,128)S(1)} %get-tuple-element.132), channel_id=1, source_target_pairs={{0,1},{1,2},{2,3},{3,4},{4,5},{5,6},{6,7},{7,8},{8,9},{9,10},{10,1... | collective-permute-start | bytes 440 | tf_op jit(solution)/shard_map/ppermute | solution.py:23
  301.2 16.1 %collective-permute-start.59 = (f32[6,6,1]{2,1,0:T(8,128)S(1)}, f32[6,6,1]{2,1,0:T(8,128)S(1)}, u32[]{:S(2)}, u32[]{:S(2)}) collective-permute-start(f32[6,6,1]{2,1,0:T(8,128)S(1)} %get-tuple-element.133), channel_id=1, source_target_pairs={{1,0},{2,1},{3,2},{4,3},{5,4},{6,5},{7,6},{8,7},{9,8},{10,9},{11,1... | collective-permute-start | bytes 440 | tf_op jit(solution)/shard_map/ppermute | solution.py:25
  309.2 9.0 %collective-permute-start.64 = (f32[6,6,1]{2,1,0:T(8,128)S(1)}, f32[6,6,1]{2,1,0:T(8,128)S(1)}, u32[]{:S(2)}, u32[]{:S(2)}) collective-permute-start(f32[6,6,1]{2,1,0:T(8,128)S(1)} %get-tuple-element.134), channel_id=1, source_target_pairs={{0,1},{1,2},{2,3},{3,4},{4,5},{5,6},{6,7},{7,8},{8,9},{9,10},{10,1... | collective-permute-start | bytes 440 | tf_op jit(solution)/shard_map/ppermute | solution.py:23
  336.4 8.3 %collective-permute-start.70 = (f32[6,6,1]{2,1,0:T(8,128)S(1)}, f32[6,6,1]{2,1,0:T(8,128)S(1)}, u32[]{:S(2)}, u32[]{:S(2)}) collective-permute-start(f32[6,6,1]{2,1,0:T(8,128)S(1)} %get-tuple-element.130), channel_id=1, source_target_pairs={{0,1},{1,2},{2,3},{3,4},{4,5},{5,6},{6,7},{7,8},{8,9},{9,10},{10,1... | collective-permute-start | bytes 440 | tf_op jit(solution)/shard_map/ppermute | solution.py:23
  433.4 8.4 %collective-permute-start.76 = (f32[10,10,1]{2,1,0:T(8,128)S(1)}, f32[10,10,1]{2,1,0:T(8,128)S(1)}, u32[]{:S(2)}, u32[]{:S(2)}) collective-permute-start(f32[10,10,1]{2,1,0:T(8,128)S(1)} %get-tuple-element.82), channel_id=1, source_target_pairs={{0,1},{1,2},{2,3},{3,4},{4,5},{5,6},{6,7},{7,8},{8,9},{9,10},{10,1... | collective-permute-start | bytes 1208 | tf_op jit(solution)/shard_map/ppermute | solution.py:23
  460.6 6.4 %collective-permute-start.82 = (f32[10,10,1]{2,1,0:T(8,128)S(1)}, f32[10,10,1]{2,1,0:T(8,128)S(1)}, u32[]{:S(2)}, u32[]{:S(2)}) collective-permute-start(f32[10,10,1]{2,1,0:T(8,128)S(1)} %get-tuple-element.80), channel_id=1, source_target_pairs={{0,1},{1,2},{2,3},{3,4},{4,5},{5,6},{6,7},{7,8},{8,9},{9,10},{10,1... | collective-permute-start | bytes 1208 | tf_op jit(solution)/shard_map/ppermute | solution.py:23
  471.0 6.2 %collective-permute-start.84 = (f32[1,8,64]{2,1,0:T(8,128)S(1)}, f32[1,8,64]{2,1,0:T(8,128)S(1)}, u32[]{:S(2)}, u32[]{:S(2)}) collective-permute-start(f32[1,8,64]{2,1,0:T(8,128)S(1)} %get-tuple-element.114), channel_id=1, source_target_pairs={{0,64},{64,128},{128,192},{192,256},{256,320},{320,384},{384,448},... | collective-permute-start | bytes 6152 | tf_op jit(solution)/shard_map/ppermute | solution.py:23
  488.0 6.4 %collective-permute-start.88 = (f32[10,10,1]{2,1,0:T(8,128)S(1)}, f32[10,10,1]{2,1,0:T(8,128)S(1)}, u32[]{:S(2)}, u32[]{:S(2)}) collective-permute-start(f32[10,10,1]{2,1,0:T(8,128)S(1)} %get-tuple-element.78), channel_id=1, source_target_pairs={{0,1},{1,2},{2,3},{3,4},{4,5},{5,6},{6,7},{7,8},{8,9},{9,10},{10,1... | collective-permute-start | bytes 1208 | tf_op jit(solution)/shard_map/ppermute | solution.py:23
  512.5 6.6 %collective-permute-start.94 = (f32[10,10,1]{2,1,0:T(8,128)S(1)}, f32[10,10,1]{2,1,0:T(8,128)S(1)}, u32[]{:S(2)}, u32[]{:S(2)}) collective-permute-start(f32[10,10,1]{2,1,0:T(8,128)S(1)} %get-tuple-element.76), channel_id=1, source_target_pairs={{0,1},{1,2},{2,3},{3,4},{4,5},{5,6},{6,7},{7,8},{8,9},{9,10},{10,1... | collective-permute-start | bytes 1208 | tf_op jit(solution)/shard_map/ppermute | solution.py:23
  541.1 7.9 %collective-permute-start.100 = (f32[20,20,2]{2,1,0:T(8,128)S(1)}, f32[20,20,2]{2,1,0:T(8,128)S(1)}, u32[]{:S(2)}, u32[]{:S(2)}) collective-permute-start(f32[20,20,2]{2,1,0:T(8,128)S(1)} %get-tuple-element.44), channel_id=1, source_target_pairs={{0,1},{1,2},{2,3},{3,4},{4,5},{5,6},{6,7},{7,8},{8,9},{9,10},{10,1... | collective-permute-start | bytes 9608 | tf_op jit(solution)/shard_map/ppermute | solution.py:23
  545.9 7.5 %collective-permute-start.101 = (f32[20,20,2]{2,1,0:T(8,128)S(1)}, f32[20,20,2]{2,1,0:T(8,128)S(1)}, u32[]{:S(2)}, u32[]{:S(2)}) collective-permute-start(f32[20,20,2]{2,1,0:T(8,128)S(1)} %get-tuple-element.45), channel_id=1, source_target_pairs={{1,0},{2,1},{3,2},{4,3},{5,4},{6,5},{7,6},{8,7},{9,8},{10,9},{11,1... | collective-permute-start | bytes 9608 | tf_op jit(solution)/shard_map/ppermute | solution.py:25
  570.6 7.6 %collective-permute-start.106 = (f32[20,20,2]{2,1,0:T(8,128)S(1)}, f32[20,20,2]{2,1,0:T(8,128)S(1)}, u32[]{:S(2)}, u32[]{:S(2)}) collective-permute-start(f32[20,20,2]{2,1,0:T(8,128)S(1)} %get-tuple-element.42), channel_id=1, source_target_pairs={{0,1},{1,2},{2,3},{3,4},{4,5},{5,6},{6,7},{7,8},{8,9},{9,10},{10,1... | collective-permute-start | bytes 9608 | tf_op jit(solution)/shard_map/ppermute | solution.py:23
  575.1 7.5 %collective-permute-start.107 = (f32[20,20,2]{2,1,0:T(8,128)S(1)}, f32[20,20,2]{2,1,0:T(8,128)S(1)}, u32[]{:S(2)}, u32[]{:S(2)}) collective-permute-start(f32[20,20,2]{2,1,0:T(8,128)S(1)} %get-tuple-element.43), channel_id=1, source_target_pairs={{1,0},{2,1},{3,2},{4,3},{5,4},{6,5},{7,6},{8,7},{9,8},{10,9},{11,1... | collective-permute-start | bytes 9608 | tf_op jit(solution)/shard_map/ppermute | solution.py:25
  (80 other events, 926.6 us)
where the time goes:
time: 597 us; the launch traced here: 587 us
  starting transfers between devices  290 us (49%)
  waiting for transfers between devices  149 us (25%)
  blocking collectives  62.5 us (10%)
  other arithmetic  41.3 us (7%)
  local copies, waits for them, and re-layouts  35.1 us (6%)
  between operations  7.9 us (1%)
    ppermute x54, starting transfers between devices, with_halo(): lax.ppermute(tail, axis, [(i, (i + 1) % count) for i in range(ends)])  195 us
    ppermute x54, waiting for transfers between devices, with_halo(): lax.ppermute(head, axis, [((i + 1) % count, i) for i in range(ends)])  143 us
    ppermute x54, starting transfers between devices, with_halo(): lax.ppermute(head, axis, [((i + 1) % count, i) for i in range(ends)])  81.8 us
    psum x4, blocking collectives, one_axis_at_a_time(): value = lax.psum(value, axis)  62.5 us
    reshape x3, local copies, waits for them, and re-layouts, coarsen(): values.reshape(extent_first // 2, 2, extent_second // 2, 2, extent_third...  22.2 us
    all_to_all x1, starting transfers between devices, move_boxes(): lax.all_to_all(ranked, GZ, split_axis=0, concat_axis=0, tiled=True)  12.9 us
  transfers between devices with their start and end apart: 109, of which 50 were waited for; matrix products, arithmetic and copies ran while one was open for 6% of the time, Pallas kernels for 0%

commit v1 on v0

v1 whole, which is shorter than its diff:
```python
import functools

import jax
import jax.numpy as jnp
from jax import lax
from jax.experimental import pallas as pl
from jax.experimental.pallas import tpu as pltpu
from jax.sharding import PartitionSpec as P

BOX = 16
NB = 8
SEND = 2
LANES = 128
MESH = pl.DeviceIdType.MESH
F32 = jnp.float32
HI = lax.Precision.HIGHEST


def iota(shape, dim):
    return lax.broadcasted_iota(jnp.int32, shape, dim)


def place(axis, step):
    count = lax.axis_size(axis)
    return {axis: lax.rem(lax.axis_index(axis) + (step + count) % count, count)}


def remote(src, dst, send, recv, axis, step):
    return pltpu.make_async_remote_copy(
        src_ref=src,
        dst_ref=dst,
        send_sem=send,
        recv_sem=recv,
        device_id=place(axis, step),
        device_id_type=MESH,
    )


def edge_scale(axis, step):
    count = lax.axis_size(axis)
    at_edge = lax.axis_index(axis) == (0 if step < 0 else count - 1)
    return jnp.where(at_edge, 0.0, 1.0).astype(F32)


class Exchange:
    def __init__(self, send, recv, base):
        self.sems = [(send.at[base + i], recv.at[base + i]) for i in range(6)]
        self.flying = []

    def pair(self, at, axis, up_src, up_dst, down_src, down_dst):
        self.flying = [
            remote(up_src, up_dst, *self.sems[at], axis, 1),
            remote(down_src, down_dst, *self.sems[at + 1], axis, -1),
        ]
        for copy in self.flying:
            copy.start()

    def land(self):
        for copy in self.flying:
            copy.wait()


class Fine(Exchange):
    def __init__(self, array, packed, z_in, y_in, *sems):
        super().__init__(*sems)
        self.array, self.packed, self.z_in, self.y_in = array, packed, z_in, y_in

    def z_start(self):
        lane = iota((16, LANES), 1)
        packed = jnp.zeros((16, LANES), F32)
        for x in range(16):
            rolled = pltpu.roll(self.array[4 + x, 0:16, 0:LANES], (8 * x + 4) % LANES, 1)
            packed = jnp.where(lane // 8 == x, rolled, packed)
        self.packed[...] = packed
        self.pair(0, "gz", self.packed, self.z_in.at[0], self.packed, self.z_in.at[1])

    def z_finish(self, mask):
        self.land()
        lower, upper = self.z_in[0], self.z_in[1]
        if mask:
            lower, upper = lower * edge_scale("gz", -1), upper * edge_scale("gz", 1)
        both = jnp.where(iota((16, LANES), 1) % 8 < 4, lower, upper)
        for x in range(16):
            self.array[4 + x, 0:16, LANES:] = pltpu.roll(both, (2 * LANES - 8 * x - 4) % LANES, 1)

    def y_start(self):
        rows = self.array.at[pl.ds(4, 16)]
        self.pair(
            2,
            "gy",
            rows.at[:, pl.ds(8, 8), :],
            self.y_in.at[0],
            rows.at[:, pl.ds(0, 8), :],
            self.y_in.at[1],
        )

    def y_finish(self, mask):
        self.land()
        low_scale = edge_scale("gy", -1) if mask else None
        high_scale = edge_scale("gy", 1) if mask else None

        def body(x, _):
            lower, upper = self.y_in[0, x], self.y_in[1, x]
            if mask:
                lower, upper = lower * low_scale, upper * high_scale
            self.array[4 + x, 16:24, :] = jnp.where(iota((8, 256), 0) < 4, upper, lower)
            return 0

        lax.fori_loop(0, 16, body, 0)

    def x_start(self):
        a = self.array
        self.pair(
            4, "gx", a.at[pl.ds(16, 4)], a.at[pl.ds(0, 4)], a.at[pl.ds(4, 4)], a.at[pl.ds(20, 4)]
        )

    def x_finish(self, mask):
        self.land()
        if mask:
            self.array[0:4] = self.array[0:4] * edge_scale("gx", -1)
            self.array[20:24] = self.array[20:24] * edge_scale("gx", 1)


class Middle(Exchange):
    def __init__(self, array, z_in, *sems):
        super().__init__(*sems)
        self.array, self.z_in = array, z_in

    def z_start(self):
        own = self.array.at[pl.ds(6, 8), pl.ds(0, 8), :]
        self.pair(0, "gz", own, self.z_in.at[0], own, self.z_in.at[1])

    def z_finish(self, mask):
        self.land()
        lane = iota((8, LANES), 1)
        for x in range(8):
            lower, upper = self.z_in[0, x], self.z_in[1, x]
            if mask:
                lower, upper = lower * edge_scale("gz", -1), upper * edge_scale("gz", 1)
            halo = pltpu.roll(jnp.where(lane < 32, upper, lower), 64, 1)
            self.array[6 + x, 0:8, :] = jnp.where(lane < 64, self.array[6 + x, 0:8, :], halo)

    def y_start(self):
        rows = self.array.at[pl.ds(6, 8)]
        own = rows.at[:, pl.ds(0, 8), :]
        self.pair(2, "gy", own, rows.at[:, pl.ds(16, 8), :], own, rows.at[:, pl.ds(8, 8), :])

    def y_finish(self, mask):
        self.land()
        if mask:
            self.array[6:14, 16:24, :] = self.array[6:14, 16:24, :] * edge_scale("gy", -1)
            self.array[6:14, 8:16, :] = self.array[6:14, 8:16, :] * edge_scale("gy", 1)

    def x_start(self):
        a = self.array
        self.pair(
            4, "gx", a.at[pl.ds(8, 6)], a.at[pl.ds(0, 6)], a.at[pl.ds(6, 6)], a.at[pl.ds(14, 6)]
        )

    def x_finish(self, mask):
        self.land()
        if mask:
            self.array[0:6] = self.array[0:6] * edge_scale("gx", -1)
            self.array[14:20] = self.array[14:20] * edge_scale("gx", 1)


class Low(Exchange):
    def __init__(self, array, z_in, y_in, *sems):
        super().__init__(*sems)
        self.array, self.z_in, self.y_in = array, z_in, y_in

    def z_start(self):
        own = self.array.at[pl.ds(4, 4), pl.ds(0, 8), :]
        self.pair(0, "gz", own, self.z_in.at[0], own, self.z_in.at[1])

    def z_finish(self, mask):
        self.land()
        lane = iota((8, LANES), 1)
        for x in range(4):
            lower, upper = self.z_in[0, x], self.z_in[1, x]
            if mask:
                lower, upper = lower * edge_scale("gz", -1), upper * edge_scale("gz", 1)
            halo = jnp.where(lane < 64, pltpu.roll(upper, 32, 1), pltpu.roll(lower, 96, 1))
            self.array[4 + x, 0:8, :] = jnp.where(lane < 32, self.array[4 + x, 0:8, :], halo)

    def y_start(self):
        own = self.array.at[pl.ds(4, 4), pl.ds(0, 8), :]
        self.pair(2, "gy", own, self.y_in.at[0], own, self.y_in.at[1])

    def y_finish(self, mask):
        self.land()
        sub = iota((8, LANES), 0)
        for x in range(4):
            lower, upper = self.y_in[0, x], self.y_in[1, x]
            if mask:
                lower, upper = lower * edge_scale("gy", -1), upper * edge_scale("gy", 1)
            own = self.array[4 + x, 0:8, :]
            self.array[4 + x, 0:8, :] = jnp.where(sub < 4, own, pltpu.roll(upper, 4, 0))
            self.array[4 + x, 8:16, :] = pltpu.roll(lower, 4, 0)

    def x_start(self):
        a = self.array
        self.pair(
            4, "gx", a.at[pl.ds(4, 4)], a.at[pl.ds(0, 4)], a.at[pl.ds(4, 4)], a.at[pl.ds(8, 4)]
        )

    def x_finish(self, mask):
        self.land()
        if mask:
            self.array[0:4] = self.array[0:4] * edge_scale("gx", -1)
            self.array[8:12] = self.array[8:12] * edge_scale("gx", 1)


def exchange_all(exchanges, mask):
    for name in ("z", "y", "x"):
        for exchange in exchanges:
            getattr(exchange, name + "_start")()
        for exchange in exchanges:
            getattr(exchange, name + "_finish")(mask)


def make_stencil(kappa, scaled, diagonal, inverse):
    planes, rows, lanes = kappa.shape

    def body(x, _):
        here = kappa[x]
        around = (
            kappa[x - 1],
            kappa[x + 1],
            pltpu.roll(here, 1, 0),
            pltpu.roll(here, rows - 1, 0),
            pltpu.roll(here, 1, 1),
            pltpu.roll(here, lanes - 1, 1),
        )
        faces = [0.5 * (here + other) for other in around]
        total = faces[0] + faces[1] + faces[2] + faces[3] + faces[4] + faces[5]
        inside = here > 0.0
        inv = jnp.where(inside, 1.0 / total, 0.0)
        diagonal[x] = jnp.where(inside, total, 0.0)
        inverse[x] = inv
        for at in range(6):
            scaled[at, x] = faces[at] * inv
        return 0

    lax.fori_loop(1, planes - 1, body, 0)


def around_sum(scaled, values, x, rows, lanes):
    here = values[x]
    total = scaled[0, x] * values[x - 1] + scaled[1, x] * values[x + 1]
    total += scaled[2, x] * pltpu.roll(here, 1, 0)
    total += scaled[3, x] * pltpu.roll(here, rows - 1, 0)
    total += scaled[4, x] * pltpu.roll(here, 1, 1)
    total += scaled[5, x] * pltpu.roll(here, lanes - 1, 1)
    return here, total


def half_sweep(scaled, low, high, colour, pairs):
    rows, lanes = scaled.shape[2:]

    def body(x, _):
        chosen = (iota((rows, lanes), 0) + iota((rows, lanes), 1) + x) % 2 == colour
        for values, source in pairs:
            here, total = around_sum(scaled, values, x, rows, lanes)
            if source is not None:
                total += source[x]
            values[x] = jnp.where(chosen, total, here)
        return 0

    lax.fori_loop(low, high, body, 0)


def first_red(values, source, kappa):
    planes, rows, lanes = values.shape

    def body(x, _):
        red = (iota((rows, lanes), 0) + iota((rows, lanes), 1) + x) % 2 == 0
        kept = jnp.where(kappa[x] > 0.0, source[x], 0.0)
        source[x] = kept
        values[x] = jnp.where(red, kept, 0.0)
        return 0

    lax.fori_loop(0, planes, body, 0)


def pair_matrix():
    return jnp.where(iota((LANES, LANES), 0) // 2 == iota((LANES, LANES), 1), 1.0, 0.0).astype(F32)


def coarsen(planes, shelf):
    count = planes.shape[0] // 2
    rows = planes.shape[1]
    halves = planes.reshape(count, 2, rows, LANES)
    summed = halves[:, 0] + halves[:, 1]
    shelf[0:count, 0:rows, :] = summed
    if rows == 8:
        shelf[0:count, 8:16, :] = jnp.zeros((count, 8, LANES), F32)
    even = shelf[0:count, pl.ds(0, 8, stride=2), :]
    odd = shelf[0:count, pl.ds(1, 8, stride=2), :]
    flat = (even + odd).reshape(count * 8, LANES)
    out = jnp.dot(flat, pair_matrix(), precision=HI, preferred_element_type=F32)
    return 0.125 * out.reshape(count, 8, LANES)


def refine_low(values, shelf, target):
    coarse, lane = iota((LANES, LANES), 0), iota((LANES, LANES), 1)
    wanted = jnp.where(lane < 96, lane // 2, 64 + lane // 2)
    matrix = jnp.where(coarse == wanted, 1.0, 0.0).astype(F32)
    flat = values.reshape(12 * 16, LANES)
    wide = jnp.dot(flat, matrix, precision=HI, preferred_element_type=F32).reshape(12, 16, LANES)
    for x in range(12):
        for odd in range(2):
            shelf[x, pl.ds(odd, 8, stride=2), :] = wide[x, 0:8]
            shelf[x, pl.ds(16 + odd, 4, stride=2), :] = wide[x, 12:16]
    for x in range(20):
        target[x] = shelf[(x + 2) // 2]


def refine_middle(values, narrow, shelf, target, added, kappa):
    coarse, lane = iota((LANES, 2 * LANES), 0), iota((LANES, 2 * LANES), 1)
    matrix = jnp.where(coarse == lane // 2, 1.0, 0.0).astype(F32)
    sub = iota((8, LANES), 0)
    for x in range(12):
        narrow[x, 0:8, :] = values[4 + x, 0:8, :]
        tail = jnp.where(sub < 2, values[4 + x, 8:16, :], pltpu.roll(values[4 + x, 16:24, :], 4, 0))
        narrow[x, 8:16, :] = tail
    flat = narrow[...].reshape(12 * 16, LANES)
    wide = jnp.dot(flat, matrix, precision=HI, preferred_element_type=F32).reshape(12, 16, 256)
    for x in range(12):
        for half in range(2):
            part = wide[x, :, half * LANES : (half + 1) * LANES]
            for odd in range(2):
                shelf[half, x, pl.ds(odd, 8, stride=2), :] = part[0:8]
                shelf[half, x, pl.ds(16 + odd, 4, stride=2), :] = part[8:12]
    for x in range(24):
        for half in range(2):
            lanes = slice(half * LANES, (half + 1) * LANES)
            fresh = shelf[half, x // 2]
            if added is not None:
                fresh = jnp.where(kappa[x, :, lanes] > 0.0, fresh + added[x, :, lanes], 0.0)
            target[x, :, lanes] = fresh


def pack_boxes(slots, ids, stage, boxes, outgoing):
    for piece in range(32):
        stage[piece * 16 : (piece + 1) * 16, :] = slots[
            0, 0, :, piece * LANES : (piece + 1) * LANES
        ].astype(F32)
    for slot in range(16):
        boxes[slot] = stage[pl.ds(slot, 32, stride=16), :].astype(jnp.bfloat16)
    held = [ids[0, 0, slot] for slot in range(16)]
    targets = [lax.shift_right_arithmetic(box, 3) for box in held]
    keys = [box * 16 + slot for slot, box in enumerate(held)]

    def body(group, _):
        least, most = jnp.int32(1 << 20), jnp.int32(0)
        for target, key in zip(targets, keys):
            here = target == group
            least = jnp.where(here, jnp.minimum(least, key), least)
            most = jnp.where(here, jnp.maximum(most, key), most)
        outgoing[2 * group] = boxes[jnp.bitwise_and(least, 15)]
        outgoing[2 * group + 1] = boxes[jnp.bitwise_and(most, 15)]
        return 0

    lax.fori_loop(0, outgoing.shape[0] // SEND, body, 0)


def unpack_boxes(incoming, owner, shelf, source):
    me = lax.axis_index("gz")
    owners = [owner[0, 0, me * NB + at] for at in range(NB)]
    planes = []
    for at in range(NB):
        rank = jnp.int32(0)
        for before in range(at):
            rank = jnp.where(owners[before] == owners[at], 1, rank)
        planes.append(incoming[owners[at] * SEND + rank].astype(F32))
    group = iota((32, LANES), 1) // BOX
    for row in range(8):
        merged = jnp.zeros((32, LANES), F32)
        for at in range(NB):
            rolled = pltpu.roll(planes[at], (BOX * (at - row)) % LANES, 1)
            merged = jnp.where(group == at, rolled, merged)
        shelf[row * 32 : (row + 1) * 32, :] = merged
    for x in range(16):
        for half in range(2):
            source[x, half * 8 : half * 8 + 8, :] = shelf[pl.ds(2 * x + half, 8, stride=32), :]


class AllSum:
    def __init__(self, axis, out, into, send, recv, base):
        self.axis, self.out, self.into = axis, out, into
        self.count = lax.axis_size(axis)
        self.send, self.recv, self.base = send, recv, base

    def start(self, tile):
        self.out[...] = tile
        self.flying = []
        for step in range(1, self.count):
            sems = (self.send.at[self.base + step], self.recv.at[self.base + step])
            copy = remote(self.out, self.into.at[step], *sems, self.axis, step)
            copy.start()
            self.flying.append(copy)

    def finish(self):
        for copy in self.flying:
            copy.wait()
        total = self.out[...]
        for step in range(1, self.count):
            total += self.into[step]
        return total


def kernel(
    slots,
    ids,
    owner,
    coefficient,
    out,
    stage,
    boxes,
    outgoing,
    incoming,
    box_shelf,
    source,
    kap0,
    kap1,
    kap2,
    sc0,
    sc1,
    sc2,
    dia0,
    dia1,
    dia2,
    inv0,
    inv1,
    inv2,
    g0,
    u0,
    w0,
    g1,
    u1,
    w1,
    f2,
    p2,
    v2,
    b1,
    c1,
    b0,
    c0,
    shelf_c,
    shelf_r1,
    narrow,
    shelf_r0,
    packed,
    z0_in,
    y0_in,
    z1_in,
    z2_in,
    y2_in,
    sum_out,
    sum_y,
    sum_z,
    sum_x,
    send,
    recv,
    box_send,
    box_recv,
    sum_send,
    sum_recv,
):
    groups = lax.axis_size("gz")
    barrier = pltpu.get_barrier_semaphore()
    partners = 0
    for axis in ("gz", "gy", "gx"):
        for step in range(1, lax.axis_size(axis)):
            pl.semaphore_signal(barrier, inc=1, device_id=place(axis, step), device_id_type=MESH)
            partners += 1

    kap0[4:20, 0:16, 0:LANES] = coefficient[...]
    mid = coarsen(coefficient[...], shelf_c)
    kap1[6:14, 0:8, :] = mid
    kap2[4:8, 0:8, :] = coarsen(mid, shelf_c)
    pack_boxes(slots, ids, stage, boxes, outgoing)

    pl.semaphore_wait(barrier, partners)

    ex_k0 = Fine(kap0, packed.at[0], z0_in.at[0], y0_in.at[0], send, recv, 0)
    ex_k1 = Middle(kap1, z1_in.at[0], send, recv, 6)
    ex_k2 = Low(kap2, z2_in.at[0], y2_in.at[0], send, recv, 12)
    kappas = (ex_k0, ex_k1, ex_k2)
    for exchange in kappas:
        exchange.z_start()

    me = lax.axis_index("gz")
    moves = []
    for step in range(1, groups):
        there = place("gz", step)["gz"]
        copy = remote(
            outgoing.at[pl.ds(SEND * there, SEND)],
            incoming.at[pl.ds(SEND * me, SEND)],
            box_send.at[step],
            box_recv.at[step],
            "gz",
            step,
        )
        copy.start()
        moves.append(copy)
    incoming[pl.ds(SEND * me, SEND)] = outgoing[pl.ds(SEND * me, SEND)]

    for exchange in kappas:
        exchange.z_finish(True)
    for name in ("y", "x"):
        for exchange in kappas:
            getattr(exchange, name + "_start")()
        for exchange in kappas:
            getattr(exchange, name + "_finish")(True)

    make_stencil(kap0, sc0, dia0, inv0)
    make_stencil(kap1, sc1, dia1, inv1)
    make_stencil(kap2, sc2, dia2, inv2)

    for copy in moves:
        copy.wait()
    unpack_boxes(incoming, owner, box_shelf, source)

    g0[4:20, 0:16, 0:LANES] = source[...] * inv0[4:20, 0:16, 0:LANES]
    exchange_all((Fine(g0, packed.at[1], z0_in.at[1], y0_in.at[1], send, recv, 18),), False)
    first_red(u0, g0, kap0)
    half_sweep(sc0, 1, 23, 1, ((u0, g0),))
    half_sweep(sc0, 2, 22, 0, ((u0, g0),))
    half_sweep(sc0, 3, 21, 1, ((u0, g0),))
    w0[4:20, 0:16, 0:LANES] = u0[4:20, 0:16, 0:LANES]

    def residual(x, _):
        here, total = around_sum(sc0, u0, x + 4, 24, 256)
        rest = dia0[x + 4] * (g0[x + 4] + total - here)
        source[x] = rest[0:16, 0:LANES]
        return 0

    lax.fori_loop(0, 16, residual, 0)

    g1[6:14, 0:8, :] = 4.0 * coarsen(source[...], shelf_c) * inv1[6:14, 0:8, :]
    ex_g1 = Middle(g1, z1_in.at[1], send, recv, 24)
    ex_w0 = Fine(w0, packed.at[2], z0_in.at[2], y0_in.at[2], send, recv, 30)
    ex_g1.z_start()
    ex_w0.z_start()
    ex_g1.z_finish(False)
    ex_g1.y_start()
    ex_w0.z_finish(False)
    ex_g1.y_finish(False)
    ex_g1.x_start()
    ex_w0.y_start()
    ex_g1.x_finish(False)
    first_red(u1, g1, kap1)
    half_sweep(sc1, 1, 19, 1, ((u1, g1),))
    half_sweep(sc1, 2, 18, 0, ((u1, g1),))
    half_sweep(sc1, 3, 17, 1, ((u1, g1),))
    w1[6:14, 0:8, :] = u1[6:14, 0:8, :]

    rests = []
    for x in range(6, 14):
        here, total = around_sum(sc1, u1, x, 24, LANES)
        rest = (0.25 * dia1[x]) * (g1[x] + total - here)
        rests.append(rest[0:8])
    f2[4:8, 0:8, :] = coarsen(jnp.stack(rests), shelf_c)
    ex_f2 = Low(f2, z2_in.at[1], y2_in.at[1], send, recv, 36)
    ex_w1 = Middle(w1, z1_in.at[2], send, recv, 42)
    ex_f2.z_start()
    ex_w1.z_start()
    ex_w0.y_finish(False)
    ex_f2.z_finish(False)
    ex_f2.y_start()
    ex_w1.z_finish(False)
    ex_w1.y_start()
    ex_f2.y_finish(False)
    ex_f2.x_start()
    ex_w0.x_start()
    ex_f2.x_finish(False)
    p2[...] = jnp.where(kap2[...] > 0.0, f2[...], 0.0)

    v2[0] = jnp.zeros((16, LANES), F32)
    v2[11] = jnp.zeros((16, LANES), F32)
    for x in range(1, 11):
        here, total = around_sum(sc2, p2, x, 16, LANES)
        v2[x] = (0.0625 * dia2[x]) * (here - total)
    own = jnp.logical_and(iota((8, LANES), 0) < 4, iota((8, LANES), 1) < 32)
    sums = [jnp.zeros((8, LANES), F32) for _ in range(6)]
    for x in range(4, 8):
        image, total = around_sum(sc2, v2, x, 16, LANES)
        second = ((0.0625 * dia2[x]) * (image - total))[0:8]
        image, here = image[0:8], p2[x, 0:8, :]
        products = (
            here * here,
            here * image,
            image * image,
            second * here,
            second * image,
            second * second,
        )
        sums = [total + jnp.where(own, product, 0.0) for total, product in zip(sums, products)]
    tile = jnp.zeros((8, LANES), F32)
    for at in range(6):
        line = jnp.sum(sums[at], axis=0, keepdims=True)
        tile = jnp.where(iota((8, LANES), 0) == at, line, tile)

    sum_gy = AllSum("gy", sum_out.at[0], sum_y, sum_send, sum_recv, 0)
    sum_gz = AllSum("gz", sum_out.at[1], sum_z, sum_send, sum_recv, lax.axis_size("gy"))
    sum_gx = AllSum(
        "gx", sum_out.at[2], sum_x, sum_send, sum_recv, lax.axis_size("gy") + groups
    )
    sum_gy.start(tile)
    ex_w1.y_finish(False)
    ex_w1.x_start()

    refine_low(p2[...], shelf_r1, b1)
    refine_low(v2[...], shelf_r1, c1)
    ex_w1.x_finish(False)
    sum_gz.start(sum_gy.finish())
    u1[...] = jnp.where(kap1[...] > 0.0, w1[...], 0.0)
    triple = ((u1, g1), (b1, None), (c1, None))
    half_sweep(sc1, 1, 19, 0, triple)
    half_sweep(sc1, 2, 18, 1, triple)
    half_sweep(sc1, 3, 17, 0, triple)
    half_sweep(sc1, 4, 16, 1, triple)

    ex_w0.x_finish(False)
    refine_middle(u1, narrow, shelf_r0, u0, w0, kap0)
    sum_gx.start(sum_gz.finish())
    refine_middle(b1, narrow, shelf_r0, b0, None, None)
    refine_middle(c1, narrow, shelf_r0, c0, None, None)
    triple = ((u0, g0), (b0, None), (c0, None))
    half_sweep(sc0, 1, 23, 0, triple)
    half_sweep(sc0, 2, 22, 1, triple)
    half_sweep(sc0, 3, 21, 0, triple)
    half_sweep(sc0, 4, 20, 1, triple)

    totals = jnp.sum(sum_gx.finish(), axis=1, keepdims=True)
    norm_rhs, along, norm_image, second_rhs, second_along, norm_second = (
        totals[at : at + 1, :] for at in range(6)
    )
    alpha = norm_rhs / along
    turned_rest = along - alpha * norm_image - alpha * second_rhs + alpha * alpha * second_along
    turned_norm = norm_image - 2.0 * alpha * second_along + alpha * alpha * norm_second
    omega = turned_rest / turned_norm
    first = jnp.broadcast_to(alpha + omega, (16, LANES))
    other = jnp.broadcast_to(alpha * omega, (16, LANES))

    def combine(x, _):
        at = (x + 4, slice(0, 16), slice(0, LANES))
        out[x] = u0[at] + first * b0[at] - other * c0[at]
        return 0

    lax.fori_loop(0, 16, combine, 0)


def solution(mesh):
    sizes = dict(mesh.shape)

    def per_device(old_slots, old_ids, old_owner, coefficient):
        vmem = pl.BlockSpec(memory_space=pltpu.VMEM)
        smem = pl.BlockSpec(memory_space=pltpu.SMEM)
        fine, middle, low = (24, 24, 256), (20, 24, 128), (12, 16, 128)
        groups = sizes["gz"]
        sums = sizes["gy"] + sizes["gz"] + sizes["gx"]
        shapes = [
            (512, LANES),
            ("b", 16, 32, LANES),
            ("b", groups * SEND, 32, LANES),
            ("b", groups * SEND, 32, LANES),
            (256, LANES),
            (16, 16, LANES),
            fine,
            middle,
            low,
            (6,) + fine,
            (6,) + middle,
            (6,) + low,
            fine,
            middle,
            low,
            fine,
            middle,
            low,
            fine,
            fine,
            fine,
            middle,
            middle,
            middle,
            low,
            low,
            low,
            middle,
            middle,
            fine,
            fine,
            (8, 16, LANES),
            (12, 24, LANES),
            (12, 16, LANES),
            (2, 12, 24, LANES),
            (3, 16, LANES),
            (3, 2, 16, LANES),
            (3, 2, 16, 8, 256),
            (3, 2, 8, 8, LANES),
            (2, 2, 4, 8, LANES),
            (2, 2, 4, 8, LANES),
            (3, 8, LANES),
            (sizes["gy"], 8, LANES),
            (sizes["gz"], 8, LANES),
            (sizes["gx"], 8, LANES),
        ]
        scratch = [
            pltpu.VMEM(shape[1:], jnp.bfloat16) if shape[0] == "b" else pltpu.VMEM(shape, F32)
            for shape in shapes
        ]
        dma = pltpu.SemaphoreType.DMA
        scratch += [dma((48,)), dma((48,)), dma((groups,)), dma((groups,))]
        scratch += [dma((sums,)), dma((sums,))]
        return pl.pallas_call(
            kernel,
            out_shape=jax.ShapeDtypeStruct(coefficient.shape, F32),
            in_specs=[vmem, smem, smem, vmem],
            out_specs=vmem,
            scratch_shapes=scratch,
            compiler_params=pltpu.CompilerParams(
                collective_id=0, has_side_effects=True, vmem_limit_bytes=48 << 20
            ),
        )(old_slots, old_ids, old_owner, coefficient)

    return jax.shard_map(
        per_device,
        mesh=mesh,
        in_specs=(
            P("gx", "gy", "gz", None),
            P("gx", "gy", "gz"),
            P("gx", "gy", None),
            P("gx", "gy", "gz"),
        ),
        out_specs=P("gx", "gy", "gz"),
        check_vma=False,
    )
```

time: 597 us -> 108 us (0.18); the launches traced: 587 us -> 108 us
  starting transfers between devices: 290 us -> 0 us
  waiting for transfers between devices: 149 us -> 0 us
  Pallas kernels: 0 us -> 104 us
  blocking collectives: 62.5 us -> 0 us
  other arithmetic: 41.3 us -> 0 us
  local copies, waits for them, and re-layouts: 35.1 us -> 3.77 us
  between operations: 7.9 us -> 0.01 us
    ppermute x108 -> x0, starting transfers between devices: 277 us -> none  [the longest x54 195 us: with_halo(): lax.ppermute(tail, axis, [(i, (i + 1) % count) for i in range(ends)])]
    ppermute x108 -> x0, waiting for transfers between devices: 149 us -> none  [the longest x54 143 us: with_halo(): lax.ppermute(head, axis, [((i + 1) % count, i) for i in range(ends)])]
    pallas_call x0 -> x1, Pallas kernels: none -> 104 us  [per_device(): pl.pallas_call(kernel, out_shape=jax.ShapeDtypeStruct(coefficient.shape,...]
    psum x4 -> x0, blocking collectives: 62.5 us -> none  [one_axis_at_a_time(): value = lax.psum(value, axis)]
    reshape x10 -> x0, local copies, waits for them, and re-layouts: 25.9 us -> none  [the longest x3 22.2 us: coarsen(): values.reshape(extent_first // 2, 2, extent_second // 2, 2, extent_third...]
    select_n x19 -> x0, other arithmetic: 13 us -> none  [the longest x14 10.8 us: relax(): return jnp.where(chosen, fresh, inner(padded))]
    all_to_all x1 -> x0, starting transfers between devices: 12.9 us -> none  [move_boxes(): lax.all_to_all(ranked, GZ, split_axis=0, concat_axis=0, tiled=True)]
    reduce_sum x7 -> x0, other arithmetic: 12.2 us -> none  [the longest x4 9.56 us: coarsen(): return grouped.mean(axis=(1, 3, 5))]
  transfers between devices with their start and end apart: 109 -> 0, of which waited for: 50 -> 0; matrix products, arithmetic and copies ran while one was open for 6% -> 0% of each run, Pallas kernels for 0% -> 0%
where the time goes in v1:
time: 108 us
  Pallas kernels  104 us (96%)
  local copies, waits for them, and re-layouts  3.77 us (3%)
    pallas_call x1, Pallas kernels, per_device(): pl.pallas_call(kernel, out_shape=jax.ShapeDtypeStruct(coefficient.shape,...  104 us
    unnamed x9, local copies, waits for them, and re-layouts  3.77 us

profile of v1, /device:TPU:1, one launch (start us, length us, event | category | flops | bytes accessed | tf_op | source)
XLA Modules:
  0.0 107.7 jit_solution(13590541546354097378)
XLA Ops:
  0.0 0.0 copy-start
  0.0 0.9 copy-done
  0.9 0.0 copy-start.1
  0.9 0.9 copy-done.1
  1.8 0.0 copy-start.2
  1.8 0.7 copy-done.2
  2.5 0.0 copy-start.3
  2.5 0.7 copy-done.3
  3.1 103.9 %shard_map.46 = f32[16,16,128]{2,1,0:T(8,128)S(1)} custom-call(bf16[1,1,16,4096]{3,2,1,0:T(8,128)(2,1)S(1)} %copy-done, s32[1,1,16]{2,1,0:T(1,128)S(1)} %copy-done.2, s32[1,1,128]{2,1,0:T(1,128)S(1)} %copy-done.3, f32[16,16,128]{2,1,0:T(8,128)S(1)} %copy-done.1), custom_call_target="tpu_custom_call" | custom-call | tf_op jit(solution)/shard_map/pallas_call | solution.py:719
  107.0 0.7 copy.6
Async XLA Ops:
  0.0 0.9 copy-start
  0.9 0.9 copy-start.1
  1.8 0.7 copy-start.2
  2.5 0.7 copy-start.3

commit v2 on v1

--- a/solution.py
+++ b/solution.py
@@ -61,64 +61,95 @@
 
 
 class Fine(Exchange):
-    def __init__(self, array, packed, z_in, y_in, *sems):
-        super().__init__(*sems)
-        self.array, self.packed, self.z_in, self.y_in = array, packed, z_in, y_in
+    def __init__(self, array, bufs, at, send, recv, base):
+        self.sems = [(send.at[base + i], recv.at[base + i]) for i in range(10)]
+        self.array, self.main = array, array.at[:, :, pl.ds(0, LANES)]
+        names = ("edge", "packed", "z_in", "y_out", "y_in", "yp_in", "xp_in")
+        for name, buf in zip(names, bufs):
+            setattr(self, name, buf.at[at])
+        self.all = {}
+
+    def pair(self, at, axis, up_src, up_dst, down_src, down_dst):
+        flying = [
+            remote(up_src, up_dst, *self.sems[at], axis, 1),
+            remote(down_src, down_dst, *self.sems[at + 1], axis, -1),
+        ]
+        for copy in flying:
+            copy.start()
+        self.all[at] = flying
+
+    def land(self, at):
+        for copy in self.all.pop(at):
+            copy.wait()
 
     def z_start(self):
-        lane = iota((16, LANES), 1)
-        packed = jnp.zeros((16, LANES), F32)
+        lane, sub = iota((16, LANES), 1), iota((8, LANES), 0)
+        edge = jnp.zeros((16, LANES), F32)
         for x in range(16):
             rolled = pltpu.roll(self.array[4 + x, 0:16, 0:LANES], (8 * x + 4) % LANES, 1)
-            packed = jnp.where(lane // 8 == x, rolled, packed)
-        self.packed[...] = packed
-        self.pair(0, "gz", self.packed, self.z_in.at[0], self.packed, self.z_in.at[1])
+            edge = jnp.where(lane // 8 == x, rolled, edge)
+        self.edge[...] = edge
+        self.pair(0, "gz", self.edge, self.z_in.at[0], self.edge, self.z_in.at[1])
+        for x in range(8):
+            near, far = self.array[4 + x, 8:16, 0:LANES], self.array[12 + x, 8:16, 0:LANES]
+            self.y_out[0, x] = jnp.where(sub < 4, pltpu.roll(far, 4, 0), near)
+            near, far = self.array[4 + x, 0:8, 0:LANES], self.array[12 + x, 0:8, 0:LANES]
+            self.y_out[1, x] = jnp.where(sub < 4, near, pltpu.roll(far, 4, 0))
+        self.pair(2, "gy", self.y_out.at[0], self.y_in.at[0], self.y_out.at[1], self.y_in.at[1])
 
     def z_finish(self, mask):
-        self.land()
+        self.land(0)
         lower, upper = self.z_in[0], self.z_in[1]
         if mask:
             lower, upper = lower * edge_scale("gz", -1), upper * edge_scale("gz", 1)
-        both = jnp.where(iota((16, LANES), 1) % 8 < 4, lower, upper)
-        for x in range(16):
-            self.array[4 + x, 0:16, LANES:] = pltpu.roll(both, (2 * LANES - 8 * x - 4) % LANES, 1)
+        self.packed[0:16, :] = jnp.where(iota((16, LANES), 1) % 8 < 4, lower, upper)
 
     def y_start(self):
-        rows = self.array.at[pl.ds(4, 16)]
-        self.pair(
-            2,
-            "gy",
-            rows.at[:, pl.ds(8, 8), :],
-            self.y_in.at[0],
-            rows.at[:, pl.ds(0, 8), :],
-            self.y_in.at[1],
-        )
+        high, low = self.packed.at[pl.ds(8, 8)], self.packed.at[pl.ds(0, 8)]
+        self.pair(4, "gy", high, self.yp_in.at[0], low, self.yp_in.at[1])
 
     def y_finish(self, mask):
-        self.land()
-        low_scale = edge_scale("gy", -1) if mask else None
-        high_scale = edge_scale("gy", 1) if mask else None
-
-        def body(x, _):
+        self.land(2)
+        low = iota((8, LANES), 0) < 4
+        scales = (edge_scale("gy", -1), edge_scale("gy", 1)) if mask else (1.0, 1.0)
+        for x in range(8):
             lower, upper = self.y_in[0, x], self.y_in[1, x]
             if mask:
-                lower, upper = lower * low_scale, upper * high_scale
-            self.array[4 + x, 16:24, :] = jnp.where(iota((8, 256), 0) < 4, upper, lower)
-            return 0
-
-        lax.fori_loop(0, 16, body, 0)
+                lower, upper = lower * scales[0], upper * scales[1]
+            self.array[4 + x, 16:24, 0:LANES] = jnp.where(low, upper, lower)
+            self.array[12 + x, 16:24, 0:LANES] = pltpu.roll(jnp.where(low, lower, upper), 4, 0)
+        main = self.main
+        self.pair(
+            6,
+            "gx",
+            main.at[pl.ds(16, 4)],
+            main.at[pl.ds(0, 4)],
+            main.at[pl.ds(4, 4)],
+            main.at[pl.ds(20, 4)],
+        )
+        self.land(4)
+        lower, upper = self.yp_in[0], self.yp_in[1]
+        if mask:
+            lower, upper = lower * scales[0], upper * scales[1]
+        self.packed[16:24, :] = jnp.where(low, upper, lower)
 
     def x_start(self):
-        a = self.array
-        self.pair(
-            4, "gx", a.at[pl.ds(16, 4)], a.at[pl.ds(0, 4)], a.at[pl.ds(4, 4)], a.at[pl.ds(20, 4)]
-        )
+        self.pair(8, "gx", self.packed, self.xp_in.at[0], self.packed, self.xp_in.at[1])
+        for x in range(16):
+            self.array[4 + x, :, LANES:] = pltpu.roll(self.packed[...], (256 - 8 * x - 4) % 128, 1)
 
     def x_finish(self, mask):
-        self.land()
+        self.land(8)
+        for x in range(4):
+            lower = pltpu.roll(self.xp_in[0], (256 - 8 * (12 + x) - 4) % LANES, 1)
+            upper = pltpu.roll(self.xp_in[1], (256 - 8 * x - 4) % LANES, 1)
+            if mask:
+                lower, upper = lower * edge_scale("gx", -1), upper * edge_scale("gx", 1)
+            self.array[x, :, LANES:], self.array[20 + x, :, LANES:] = lower, upper
+        self.land(6)
         if mask:
-            self.array[0:4] = self.array[0:4] * edge_scale("gx", -1)
-            self.array[20:24] = self.array[20:24] * edge_scale("gx", 1)
+            self.array[0:4, :, 0:LANES] = self.array[0:4, :, 0:LANES] * edge_scale("gx", -1)
+            self.array[20:24, :, 0:LANES] = self.array[20:24, :, 0:LANES] * edge_scale("gx", 1)
 
 
 class Middle(Exchange):
@@ -211,76 +242,84 @@
             self.array[8:12] = self.array[8:12] * edge_scale("gx", 1)
 
 
-def exchange_all(exchanges, mask):
-    for name in ("z", "y", "x"):
-        for exchange in exchanges:
-            getattr(exchange, name + "_start")()
-        for exchange in exchanges:
-            getattr(exchange, name + "_finish")(mask)
+def in_pieces(low, high, size, piece):
+    count = (high - low) // size
+
+    def body(at, _):
+        piece(low + at * size, size)
+        return 0
+
+    lax.fori_loop(0, count, body, 0)
+    if low + count * size < high:
+        piece(low + count * size, high - low - count * size)
 
 
 def make_stencil(kappa, scaled, diagonal, inverse):
     planes, rows, lanes = kappa.shape
 
-    def body(x, _):
-        here = kappa[x]
+    def piece(x, size):
+        wide = kappa[pl.ds(x - 1, size + 2)]
+        here = wide[1:-1]
         around = (
-            kappa[x - 1],
-            kappa[x + 1],
-            pltpu.roll(here, 1, 0),
-            pltpu.roll(here, rows - 1, 0),
+            wide[:-2],
+            wide[2:],
             pltpu.roll(here, 1, 1),
-            pltpu.roll(here, lanes - 1, 1),
+            pltpu.roll(here, rows - 1, 1),
+            pltpu.roll(here, 1, 2),
+            pltpu.roll(here, lanes - 1, 2),
         )
         faces = [0.5 * (here + other) for other in around]
         total = faces[0] + faces[1] + faces[2] + faces[3] + faces[4] + faces[5]
         inside = here > 0.0
         inv = jnp.where(inside, 1.0 / total, 0.0)
-        diagonal[x] = jnp.where(inside, total, 0.0)
-        inverse[x] = inv
+        diagonal[pl.ds(x, size)] = jnp.where(inside, total, 0.0)
+        inverse[pl.ds(x, size)] = inv
         for at in range(6):
-            scaled[at, x] = faces[at] * inv
-        return 0
-
-    lax.fori_loop(1, planes - 1, body, 0)
-
-
-def around_sum(scaled, values, x, rows, lanes):
-    here = values[x]
-    total = scaled[0, x] * values[x - 1] + scaled[1, x] * values[x + 1]
-    total += scaled[2, x] * pltpu.roll(here, 1, 0)
-    total += scaled[3, x] * pltpu.roll(here, rows - 1, 0)
-    total += scaled[4, x] * pltpu.roll(here, 1, 1)
-    total += scaled[5, x] * pltpu.roll(here, lanes - 1, 1)
+            scaled[at, pl.ds(x, size)] = faces[at] * inv
+
+    in_pieces(1, planes - 1, 2, piece)
+
+
+def around_sum(scaled, values, x, size):
+    rows, lanes = scaled.shape[2:]
+    wide = values[pl.ds(x - 1, size + 2)]
+    here = wide[1:-1]
+    face = [scaled.at[at, pl.ds(x, size)] for at in range(6)]
+    total = face[0][...] * wide[:-2] + face[1][...] * wide[2:]
+    total += face[2][...] * pltpu.roll(here, 1, 1)
+    total += face[3][...] * pltpu.roll(here, rows - 1, 1)
+    total += face[4][...] * pltpu.roll(here, 1, 2)
+    total += face[5][...] * pltpu.roll(here, lanes - 1, 2)
     return here, total
 
 
-def half_sweep(scaled, low, high, colour, pairs):
+def half_sweep(scaled, low, high, colour, pairs, size):
     rows, lanes = scaled.shape[2:]
-
-    def body(x, _):
-        chosen = (iota((rows, lanes), 0) + iota((rows, lanes), 1) + x) % 2 == colour
+    parity = (iota((rows, lanes), 0) + iota((rows, lanes), 1)) % 2
+
+    def piece(x, count):
         for values, source in pairs:
-            here, total = around_sum(scaled, values, x, rows, lanes)
+            here, total = around_sum(scaled, values, x, count)
             if source is not None:
-                total += source[x]
-            values[x] = jnp.where(chosen, total, here)
-        return 0
-
-    lax.fori_loop(low, high, body, 0)
+                total += source[pl.ds(x, count)]
+            for at in range(count):
+                chosen = parity == (low + at + colour) % 2
+                values[x + at] = jnp.where(chosen, total[at], here[at])
+
+    in_pieces(low, high, size, piece)
 
 
 def first_red(values, source, kappa):
     planes, rows, lanes = values.shape
-
-    def body(x, _):
-        red = (iota((rows, lanes), 0) + iota((rows, lanes), 1) + x) % 2 == 0
-        kept = jnp.where(kappa[x] > 0.0, source[x], 0.0)
-        source[x] = kept
-        values[x] = jnp.where(red, kept, 0.0)
-        return 0
-
-    lax.fori_loop(0, planes, body, 0)
+    parity = (iota((rows, lanes), 0) + iota((rows, lanes), 1)) % 2
+
+    def piece(x, count):
+        for at in range(count):
+            kept = jnp.where(kappa[x + at] > 0.0, source[x + at], 0.0)
+            source[x + at] = kept
+            values[x + at] = jnp.where(parity == at % 2, kept, 0.0)
+
+    in_pieces(0, planes, 4, piece)
 
 
 def pair_matrix():
@@ -411,9 +450,9 @@
 
 
 def kernel(
-    slots,
-    ids,
-    owner,
+    slots_in,
+    ids_in,
+    owner_in,
     coefficient,
     out,
     stage,
@@ -451,9 +490,13 @@
     shelf_r1,
     narrow,
     shelf_r0,
+    edge,
     packed,
     z0_in,
+    y0_out,
     y0_in,
+    yp0_in,
+    xp0_in,
     z1_in,
     z2_in,
     y2_in,
@@ -467,7 +510,19 @@
     box_recv,
     sum_send,
     sum_recv,
+    slots,
+    ids,
+    owner,
+    load_sem,
 ):
+    loads = [
+        pltpu.make_async_copy(coefficient, kap0.at[pl.ds(4, 16), pl.ds(0, 16), pl.ds(0, LANES)], load_sem.at[0]),
+        pltpu.make_async_copy(slots_in, slots, load_sem.at[1]),
+        pltpu.make_async_copy(ids_in, ids, load_sem.at[2]),
+        pltpu.make_async_copy(owner_in, owner, load_sem.at[3]),
+    ]
+    for load in loads:
+        load.start()
     groups = lax.axis_size("gz")
     barrier = pltpu.get_barrier_semaphore()
     partners = 0
@@ -476,20 +531,15 @@
             pl.semaphore_signal(barrier, inc=1, device_id=place(axis, step), device_id_type=MESH)
             partners += 1
 
-    kap0[4:20, 0:16, 0:LANES] = coefficient[...]
-    mid = coarsen(coefficient[...], shelf_c)
-    kap1[6:14, 0:8, :] = mid
-    kap2[4:8, 0:8, :] = coarsen(mid, shelf_c)
+    for load in loads:
+        load.wait()
+    fine_bufs = (edge, packed, z0_in, y0_out, y0_in, yp0_in, xp0_in)
     pack_boxes(slots, ids, stage, boxes, outgoing)
 
     pl.semaphore_wait(barrier, partners)
 
-    ex_k0 = Fine(kap0, packed.at[0], z0_in.at[0], y0_in.at[0], send, recv, 0)
-    ex_k1 = Middle(kap1, z1_in.at[0], send, recv, 6)
-    ex_k2 = Low(kap2, z2_in.at[0], y2_in.at[0], send, recv, 12)
-    kappas = (ex_k0, ex_k1, ex_k2)
-    for exchange in kappas:
-        exchange.z_start()
+    ex_k0 = Fine(kap0, fine_bufs, 0, send, recv, 0)
+    ex_k0.z_start()
 
     me = lax.axis_index("gz")
     moves = []
@@ -507,97 +557,110 @@
         moves.append(copy)
     incoming[pl.ds(SEND * me, SEND)] = outgoing[pl.ds(SEND * me, SEND)]
 
-    for exchange in kappas:
-        exchange.z_finish(True)
-    for name in ("y", "x"):
-        for exchange in kappas:
-            getattr(exchange, name + "_start")()
-        for exchange in kappas:
-            getattr(exchange, name + "_finish")(True)
-
+    mid = coarsen(kap0[4:20, 0:16, 0:LANES], shelf_c)
+    kap1[6:14, 0:8, :] = mid
+    kap2[4:8, 0:8, :] = coarsen(mid, shelf_c)
+    ex_k1 = Middle(kap1, z1_in.at[0], send, recv, 30)
+    ex_k2 = Low(kap2, z2_in.at[0], y2_in.at[0], send, recv, 36)
+    ex_k0.z_finish(True)
+    ex_k0.y_start()
+    ex_k1.z_start()
+    ex_k2.z_start()
+    ex_k0.y_finish(True)
+    ex_k0.x_start()
+    ex_k1.z_finish(True)
+    ex_k1.y_start()
+    ex_k2.z_finish(True)
+    ex_k2.y_start()
+    ex_k0.x_finish(True)
     make_stencil(kap0, sc0, dia0, inv0)
-    make_stencil(kap1, sc1, dia1, inv1)
-    make_stencil(kap2, sc2, dia2, inv2)
+    ex_k1.y_finish(True)
+    ex_k1.x_start()
+    ex_k2.y_finish(True)
+    ex_k2.x_start()
 
     for copy in moves:
         copy.wait()
     unpack_boxes(incoming, owner, box_shelf, source)
 
     g0[4:20, 0:16, 0:LANES] = source[...] * inv0[4:20, 0:16, 0:LANES]
-    exchange_all((Fine(g0, packed.at[1], z0_in.at[1], y0_in.at[1], send, recv, 18),), False)
+    ex_g0 = Fine(g0, fine_bufs, 1, send, recv, 10)
+    ex_g0.z_start()
+    ex_k1.x_finish(True)
+    ex_k2.x_finish(True)
+    ex_g0.z_finish(False)
+    ex_g0.y_start()
+    make_stencil(kap1, sc1, dia1, inv1)
+    ex_g0.y_finish(False)
+    ex_g0.x_start()
+    make_stencil(kap2, sc2, dia2, inv2)
+    ex_g0.x_finish(False)
     first_red(u0, g0, kap0)
-    half_sweep(sc0, 1, 23, 1, ((u0, g0),))
-    half_sweep(sc0, 2, 22, 0, ((u0, g0),))
-    half_sweep(sc0, 3, 21, 1, ((u0, g0),))
+    half_sweep(sc0, 1, 23, 1, ((u0, g0),), 4)
+    half_sweep(sc0, 2, 22, 0, ((u0, g0),), 4)
+    half_sweep(sc0, 3, 21, 1, ((u0, g0),), 4)
     w0[4:20, 0:16, 0:LANES] = u0[4:20, 0:16, 0:LANES]
 
-    def residual(x, _):
-        here, total = around_sum(sc0, u0, x + 4, 24, 256)
-        rest = dia0[x + 4] * (g0[x + 4] + total - here)
-        source[x] = rest[0:16, 0:LANES]
-        return 0
-
-    lax.fori_loop(0, 16, residual, 0)
+    def residual(x, count):
+        here, total = around_sum(sc0, u0, x, count)
+        rest = dia0[pl.ds(x, count)] * (g0[pl.ds(x, count)] + total - here)
+        source[pl.ds(x - 4, count)] = rest[:, 0:16, 0:LANES]
+
+    in_pieces(4, 20, 4, residual)
 
     g1[6:14, 0:8, :] = 4.0 * coarsen(source[...], shelf_c) * inv1[6:14, 0:8, :]
-    ex_g1 = Middle(g1, z1_in.at[1], send, recv, 24)
-    ex_w0 = Fine(w0, packed.at[2], z0_in.at[2], y0_in.at[2], send, recv, 30)
+    ex_g1 = Middle(g1, z1_in.at[1], send, recv, 42)
+    ex_w0 = Fine(w0, fine_bufs, 2, send, recv, 20)
     ex_g1.z_start()
-    ex_w0.z_start()
     ex_g1.z_finish(False)
     ex_g1.y_start()
-    ex_w0.z_finish(False)
     ex_g1.y_finish(False)
     ex_g1.x_start()
-    ex_w0.y_start()
+    ex_w0.z_start()
     ex_g1.x_finish(False)
     first_red(u1, g1, kap1)
-    half_sweep(sc1, 1, 19, 1, ((u1, g1),))
-    half_sweep(sc1, 2, 18, 0, ((u1, g1),))
-    half_sweep(sc1, 3, 17, 1, ((u1, g1),))
+    half_sweep(sc1, 1, 19, 1, ((u1, g1),), 6)
+    half_sweep(sc1, 2, 18, 0, ((u1, g1),), 8)
+    half_sweep(sc1, 3, 17, 1, ((u1, g1),), 14)
     w1[6:14, 0:8, :] = u1[6:14, 0:8, :]
 
-    rests = []
-    for x in range(6, 14):
-        here, total = around_sum(sc1, u1, x, 24, LANES)
-        rest = (0.25 * dia1[x]) * (g1[x] + total - here)
-        rests.append(rest[0:8])
-    f2[4:8, 0:8, :] = coarsen(jnp.stack(rests), shelf_c)
-    ex_f2 = Low(f2, z2_in.at[1], y2_in.at[1], send, recv, 36)
-    ex_w1 = Middle(w1, z1_in.at[2], send, recv, 42)
+    here, total = around_sum(sc1, u1, 6, 8)
+    rest = (0.25 * dia1[6:14]) * (g1[6:14] + total - here)
+    f2[4:8, 0:8, :] = coarsen(rest[:, 0:8], shelf_c)
+    ex_f2 = Low(f2, z2_in.at[1], y2_in.at[1], send, recv, 48)
+    ex_w1 = Middle(w1, z1_in.at[2], send, recv, 54)
     ex_f2.z_start()
     ex_w1.z_start()
-    ex_w0.y_finish(False)
     ex_f2.z_finish(False)
     ex_f2.y_start()
+    ex_w0.z_finish(False)
+    ex_w0.y_start()
     ex_w1.z_finish(False)
     ex_w1.y_start()
     ex_f2.y_finish(False)
     ex_f2.x_start()
+    ex_w0.y_finish(False)
     ex_w0.x_start()
     ex_f2.x_finish(False)
     p2[...] = jnp.where(kap2[...] > 0.0, f2[...], 0.0)
 
     v2[0] = jnp.zeros((16, LANES), F32)
     v2[11] = jnp.zeros((16, LANES), F32)
-    for x in range(1, 11):
-        here, total = around_sum(sc2, p2, x, 16, LANES)
-        v2[x] = (0.0625 * dia2[x]) * (here - total)
+    here, total = around_sum(sc2, p2, 1, 10)
+    v2[1:11] = (0.0625 * dia2[1:11]) * (here - total)
     own = jnp.logical_and(iota((8, LANES), 0) < 4, iota((8, LANES), 1) < 32)
-    sums = [jnp.zeros((8, LANES), F32) for _ in range(6)]
-    for x in range(4, 8):
-        image, total = around_sum(sc2, v2, x, 16, LANES)
-        second = ((0.0625 * dia2[x]) * (image - total))[0:8]
-        image, here = image[0:8], p2[x, 0:8, :]
-        products = (
-            here * here,
-            here * image,
-            image * image,
-            second * here,
-            second * image,
-            second * second,
-        )
-        sums = [total + jnp.where(own, product, 0.0) for total, product in zip(sums, products)]
+    image, total = around_sum(sc2, v2, 4, 4)
+    second = ((0.0625 * dia2[4:8]) * (image - total))[:, 0:8]
+    image, here = image[:, 0:8], p2[4:8, 0:8, :]
+    products = (
+        here * here,
+        here * image,
+        image * image,
+        second * here,
+        second * image,
+        second * second,
+    )
+    sums = [jnp.where(own, jnp.sum(product, axis=0), 0.0) for product in products]
     tile = jnp.zeros((8, LANES), F32)
     for at in range(6):
         line = jnp.sum(sums[at], axis=0, keepdims=True)
@@ -618,10 +681,10 @@
     sum_gz.start(sum_gy.finish())
     u1[...] = jnp.where(kap1[...] > 0.0, w1[...], 0.0)
     triple = ((u1, g1), (b1, None), (c1, None))
-    half_sweep(sc1, 1, 19, 0, triple)
-    half_sweep(sc1, 2, 18, 1, triple)
-    half_sweep(sc1, 3, 17, 0, triple)
-    half_sweep(sc1, 4, 16, 1, triple)
+    half_sweep(sc1, 1, 19, 0, triple, 6)
+    half_sweep(sc1, 2, 18, 1, triple, 8)
+    half_sweep(sc1, 3, 17, 0, triple, 14)
+    half_sweep(sc1, 4, 16, 1, triple, 6)
 
     ex_w0.x_finish(False)
     refine_middle(u1, narrow, shelf_r0, u0, w0, kap0)
@@ -629,10 +692,10 @@
     refine_middle(b1, narrow, shelf_r0, b0, None, None)
     refine_middle(c1, narrow, shelf_r0, c0, None, None)
     triple = ((u0, g0), (b0, None), (c0, None))
-    half_sweep(sc0, 1, 23, 0, triple)
-    half_sweep(sc0, 2, 22, 1, triple)
-    half_sweep(sc0, 3, 21, 0, triple)
-    half_sweep(sc0, 4, 20, 1, triple)
+    half_sweep(sc0, 1, 23, 0, triple, 4)
+    half_sweep(sc0, 2, 22, 1, triple, 4)
+    half_sweep(sc0, 3, 21, 0, triple, 4)
+    half_sweep(sc0, 4, 20, 1, triple, 4)
 
     totals = jnp.sum(sum_gx.finish(), axis=1, keepdims=True)
     norm_rhs, along, norm_image, second_rhs, second_along, norm_second = (
@@ -658,7 +721,7 @@
 
     def per_device(old_slots, old_ids, old_owner, coefficient):
         vmem = pl.BlockSpec(memory_space=pltpu.VMEM)
-        smem = pl.BlockSpec(memory_space=pltpu.SMEM)
+        far = pl.BlockSpec(memory_space=pltpu.HBM)
         fine, middle, low = (24, 24, 256), (20, 24, 128), (12, 16, 128)
         groups = sizes["gz"]
         sums = sizes["gy"] + sizes["gz"] + sizes["gx"]
@@ -699,8 +762,12 @@
             (12, 16, LANES),
             (2, 12, 24, LANES),
             (3, 16, LANES),
+            (3, 24, LANES),
             (3, 2, 16, LANES),
-            (3, 2, 16, 8, 256),
+            (3, 2, 8, 8, LANES),
+            (3, 2, 8, 8, LANES),
+            (3, 2, 8, LANES),
+            (3, 2, 24, LANES),
             (3, 2, 8, 8, LANES),
             (2, 2, 4, 8, LANES),
             (2, 2, 4, 8, LANES),
@@ -714,16 +781,18 @@
             for shape in shapes
         ]
         dma = pltpu.SemaphoreType.DMA
-        scratch += [dma((48,)), dma((48,)), dma((groups,)), dma((groups,))]
+        scratch += [dma((60,)), dma((60,)), dma((groups,)), dma((groups,))]
         scratch += [dma((sums,)), dma((sums,))]
+        scratch += [pltpu.VMEM(old_slots.shape, jnp.bfloat16), pltpu.SMEM(old_ids.shape, jnp.int32)]
+        scratch += [pltpu.SMEM(old_owner.shape, jnp.int32), dma((4,))]
         return pl.pallas_call(
             kernel,
             out_shape=jax.ShapeDtypeStruct(coefficient.shape, F32),
-            in_specs=[vmem, smem, smem, vmem],
+            in_specs=[far] * 4,
             out_specs=vmem,
             scratch_shapes=scratch,
             compiler_params=pltpu.CompilerParams(
-                collective_id=0, has_side_effects=True, vmem_limit_bytes=48 << 20
+                collective_id=0, has_side_effects=True, vmem_limit_bytes=67_000_000
             ),
         )(old_slots, old_ids, old_owner, coefficient)
 

time: 108 us -> 84.1 us (0.78)
  Pallas kernels: 104 us -> 82.3 us
  local copies, waits for them, and re-layouts: 3.77 us -> 1.57 us
    pallas_call x1, Pallas kernels: 104 us -> 82.3 us  [per_device(): pl.pallas_call(kernel, out_shape=jax.ShapeDtypeStruct(coefficient.shape,...]
    unnamed x9 -> x1, local copies, waits for them, and re-layouts: 3.77 us -> 1.57 us
where the time goes in v2:
time: 84.1 us; the launch traced here: 83.9 us
  Pallas kernels  82.3 us (98%)
  local copies, waits for them, and re-layouts  1.57 us (2%)
    pallas_call x1, Pallas kernels, per_device(): pl.pallas_call(kernel, out_shape=jax.ShapeDtypeStruct(coefficient.shape,...  82.3 us

profile of v2, /device:TPU:1, one launch (start us, length us, event | category | flops | bytes accessed | tf_op | source)
XLA Modules:
  0.0 83.9 jit_solution(15149575848421143213)
XLA Ops:
  0.0 82.3 %shard_map.46 = f32[16,16,128]{2,1,0:T(8,128)} custom-call(bf16[1,1,16,4096]{3,2,1,0:T(8,128)(2,1)} %slots_in.1, s32[1,1,16]{2,1,0:T(1,128)} %ids_in.1, s32[1,1,128]{2,1,0:T(1,128)} %owner_in.1, f32[16,16,128]{2,1,0:T(8,128)} %coefficient.1), custom_call_target="tpu_custom_call" | custom-call | tf_op jit(solution)/shard_map/pallas_call | solution.py:788
  82.3 1.6 %copy.6 = f32[16,16,128]{2,1,0:T(8,128)} copy(f32[16,16,128]{2,1,0:T(8,128)} %shard_map.46) | data formatting | bytes 262144

commit v3 on v2

--- a/solution.py
+++ b/solution.py
@@ -42,25 +42,137 @@
     return jnp.where(at_edge, 0.0, 1.0).astype(F32)
 
 
-class Exchange:
-    def __init__(self, send, recv, base):
-        self.sems = [(send.at[base + i], recv.at[base + i]) for i in range(6)]
+NEAR = [(dx, dy, 0) for dx in (-1, 0, 1) for dy in (-1, 0, 1) if (dx, dy) != (0, 0)]
+ENDS = [(dx, dy, dz) for dx in (-1, 0, 1) for dy in (-1, 0, 1) for dz in (-1, 1)]
+
+
+def block(dx, dy):
+    return 3 * (dx + 1) + dy + 1
+
+
+def spot(dx, dy, dz):
+    return {**place("gx", dx), **place("gy", dy), **place("gz", dz)}
+
+
+class Direct:
+    def begin(self, send, recv, base, plan):
         self.flying = []
-
-    def pair(self, at, axis, up_src, up_dst, down_src, down_dst):
-        self.flying = [
-            remote(up_src, up_dst, *self.sems[at], axis, 1),
-            remote(down_src, down_dst, *self.sems[at + 1], axis, -1),
-        ]
-        for copy in self.flying:
+        for at, (offset, src, dst) in enumerate(plan):
+            copy = pltpu.make_async_remote_copy(
+                src_ref=src,
+                dst_ref=dst,
+                send_sem=send.at[base + at],
+                recv_sem=recv.at[base + at],
+                device_id=spot(*offset),
+                device_id_type=MESH,
+            )
             copy.start()
+            self.flying.append(copy)
 
     def land(self):
         for copy in self.flying:
             copy.wait()
 
 
-class Fine(Exchange):
+def scales_of(mask):
+    if not mask:
+        return None
+    return {axis: {-1: edge_scale(axis, -1), 1: edge_scale(axis, 1)} for axis in ("gx", "gy", "gz")}
+
+
+def scaled_by(value, scales, dx, dy, dz):
+    if scales is None:
+        return value
+    for axis, step in (("gx", dx), ("gy", dy), ("gz", dz)):
+        if step:
+            value = value * scales[axis][step]
+    return value
+
+
+class Middle(Direct):
+    def __init__(self, array, bufs, at, send, recv, base):
+        self.array, self.where = array, (send, recv, base)
+        self.edge, self.main_in, self.edge_in = (buf.at[at] for buf in bufs)
+
+    def start(self, own):
+        lane = iota((8, LANES), 1)
+        mirrored = pltpu.roll(own, 64, 2)
+        both = own + mirrored
+        edge = jnp.zeros((8, LANES), F32)
+        for x in range(8):
+            edge = jnp.where(lane // 16 == x, pltpu.roll(both[x], (16 * x + 8) % LANES, 1), edge)
+        self.edge[...] = edge
+        mine = self.main_in.at[block(0, 0)]
+        for x in range(4):
+            mine[x] = own[x] + mirrored[x + 4]
+        plan = [
+            ((dx, dy, dz), self.edge, self.edge_in.at[(1 - dz) // 2, block(-dx, -dy)])
+            for dx, dy, dz in ENDS
+        ]
+        plan += [
+            ((dx, dy, dz), mine, self.main_in.at[block(-dx, -dy)]) for dx, dy, dz in NEAR
+        ]
+        self.begin(*self.where, plan)
+
+    def finish(self, mask):
+        self.land()
+        scales = scales_of(mask)
+        lane = iota((8, LANES), 1)
+        for dx, planes, first in ((-1, range(2, 8), 0), (0, range(8), 6), (1, range(6), 14)):
+            for dy, row in ((0, 0), (1, 8), (-1, 16)):
+                main = self.main_in.at[block(dx, dy)]
+                lower = scaled_by(self.edge_in[0, block(dx, dy)], scales, dx, dy, -1)
+                upper = scaled_by(self.edge_in[1, block(dx, dy)], scales, dx, dy, 1)
+                for at, x in enumerate(planes):
+                    own = main[x % 4] if x < 4 else pltpu.roll(main[x % 4], 64, 1)
+                    own = scaled_by(own, scales, dx, dy, 0)
+                    high = pltpu.roll(upper, (56 - 16 * x) % LANES, 1)
+                    low = pltpu.roll(lower, (120 - 16 * x) % LANES, 1)
+                    halo = jnp.where(lane < 96, high, low)
+                    self.array[first + at, row : row + 8, :] = jnp.where(lane < 64, own, halo)
+
+
+class Low(Direct):
+    def __init__(self, array, bufs, at, send, recv, base):
+        self.array, self.where = array, (send, recv, base)
+        (self.tiles,) = (buf.at[at] for buf in bufs)
+
+    def start(self, own):
+        lane = iota((8, LANES), 1)
+        tile = jnp.zeros((8, LANES), F32)
+        for x in range(4):
+            tile = jnp.where(lane // 32 == x, pltpu.roll(own[x], (32 * x) % LANES, 1), tile)
+        mine = self.tiles.at[1, block(0, 0)]
+        mine[...] = tile
+        plan = [
+            ((dx, dy, dz), mine, self.tiles.at[1 - dz, block(-dx, -dy)])
+            for dx, dy, dz in ENDS + NEAR
+        ]
+        self.begin(*self.where, plan)
+
+    def finish(self, mask):
+        self.land()
+        scales = scales_of(mask)
+        lane, sub = iota((8, LANES), 1), iota((8, LANES), 0)
+        for dx in (-1, 0, 1):
+            firsts, seconds = [], []
+            for dz in (-1, 0, 1):
+                here, above, below = (
+                    scaled_by(self.tiles[dz + 1, block(dx, dy)], scales, dx, dy, dz)
+                    for dy in (0, 1, -1)
+                )
+                firsts.append(jnp.where(sub < 4, here, pltpu.roll(above, 4, 0)))
+                seconds.append(jnp.where(sub < 4, 0.0, pltpu.roll(below, 4, 0)))
+            for x in range(4):
+                for row, parts in ((0, firsts), (8, seconds)):
+                    low = pltpu.roll(parts[0], (96 - 32 * x) % LANES, 1)
+                    own = pltpu.roll(parts[1], (128 - 32 * x) % LANES, 1)
+                    high = pltpu.roll(parts[2], (160 - 32 * x) % LANES, 1)
+                    halo = jnp.where(lane < 64, high, low)
+                    self.array[4 + 4 * dx + x, row : row + 8, :] = jnp.where(lane < 32, own, halo)
+
+
+class Fine:
     def __init__(self, array, bufs, at, send, recv, base):
         self.sems = [(send.at[base + i], recv.at[base + i]) for i in range(10)]
         self.array, self.main = array, array.at[:, :, pl.ds(0, LANES)]
@@ -150,96 +262,6 @@
         if mask:
             self.array[0:4, :, 0:LANES] = self.array[0:4, :, 0:LANES] * edge_scale("gx", -1)
             self.array[20:24, :, 0:LANES] = self.array[20:24, :, 0:LANES] * edge_scale("gx", 1)
-
-
-class Middle(Exchange):
-    def __init__(self, array, z_in, *sems):
-        super().__init__(*sems)
-        self.array, self.z_in = array, z_in
-
-    def z_start(self):
-        own = self.array.at[pl.ds(6, 8), pl.ds(0, 8), :]
-        self.pair(0, "gz", own, self.z_in.at[0], own, self.z_in.at[1])
-
-    def z_finish(self, mask):
-        self.land()
-        lane = iota((8, LANES), 1)
-        for x in range(8):
-            lower, upper = self.z_in[0, x], self.z_in[1, x]
-            if mask:
-                lower, upper = lower * edge_scale("gz", -1), upper * edge_scale("gz", 1)
-            halo = pltpu.roll(jnp.where(lane < 32, upper, lower), 64, 1)
-            self.array[6 + x, 0:8, :] = jnp.where(lane < 64, self.array[6 + x, 0:8, :], halo)
-
-    def y_start(self):
-        rows = self.array.at[pl.ds(6, 8)]
-        own = rows.at[:, pl.ds(0, 8), :]
-        self.pair(2, "gy", own, rows.at[:, pl.ds(16, 8), :], own, rows.at[:, pl.ds(8, 8), :])
-
-    def y_finish(self, mask):
-        self.land()
-        if mask:
-            self.array[6:14, 16:24, :] = self.array[6:14, 16:24, :] * edge_scale("gy", -1)
-            self.array[6:14, 8:16, :] = self.array[6:14, 8:16, :] * edge_scale("gy", 1)
-
-    def x_start(self):
-        a = self.array
-        self.pair(
-            4, "gx", a.at[pl.ds(8, 6)], a.at[pl.ds(0, 6)], a.at[pl.ds(6, 6)], a.at[pl.ds(14, 6)]
-        )
-
-    def x_finish(self, mask):
-        self.land()
-        if mask:
-            self.array[0:6] = self.array[0:6] * edge_scale("gx", -1)
-            self.array[14:20] = self.array[14:20] * edge_scale("gx", 1)
-
-
-class Low(Exchange):
-    def __init__(self, array, z_in, y_in, *sems):
-        super().__init__(*sems)
-        self.array, self.z_in, self.y_in = array, z_in, y_in
-
-    def z_start(self):
-        own = self.array.at[pl.ds(4, 4), pl.ds(0, 8), :]
-        self.pair(0, "gz", own, self.z_in.at[0], own, self.z_in.at[1])
-
-    def z_finish(self, mask):
-        self.land()
-        lane = iota((8, LANES), 1)
-        for x in range(4):
-            lower, upper = self.z_in[0, x], self.z_in[1, x]
-            if mask:
-                lower, upper = lower * edge_scale("gz", -1), upper * edge_scale("gz", 1)
-            halo = jnp.where(lane < 64, pltpu.roll(upper, 32, 1), pltpu.roll(lower, 96, 1))
-            self.array[4 + x, 0:8, :] = jnp.where(lane < 32, self.array[4 + x, 0:8, :], halo)
-
-    def y_start(self):
-        own = self.array.at[pl.ds(4, 4), pl.ds(0, 8), :]
-        self.pair(2, "gy", own, self.y_in.at[0], own, self.y_in.at[1])
-
-    def y_finish(self, mask):
-        self.land()
-        sub = iota((8, LANES), 0)
-        for x in range(4):
-            lower, upper = self.y_in[0, x], self.y_in[1, x]
-            if mask:
-                lower, upper = lower * edge_scale("gy", -1), upper * edge_scale("gy", 1)
-            own = self.array[4 + x, 0:8, :]
-            self.array[4 + x, 0:8, :] = jnp.where(sub < 4, own, pltpu.roll(upper, 4, 0))
-            self.array[4 + x, 8:16, :] = pltpu.roll(lower, 4, 0)
-
-    def x_start(self):
-        a = self.array
-        self.pair(
-            4, "gx", a.at[pl.ds(4, 4)], a.at[pl.ds(0, 4)], a.at[pl.ds(4, 4)], a.at[pl.ds(8, 4)]
-        )
-
-    def x_finish(self, mask):
-        self.land()
-        if mask:
-            self.array[0:4] = self.array[0:4] * edge_scale("gx", -1)
-            self.array[8:12] = self.array[8:12] * edge_scale("gx", 1)
 
 
 def in_pieces(low, high, size, piece):
@@ -497,9 +519,10 @@
     y0_in,
     yp0_in,
     xp0_in,
-    z1_in,
-    z2_in,
-    y2_in,
+    edge1,
+    main1_in,
+    edge1_in,
+    tiles2,
     sum_out,
     sum_y,
     sum_z,
@@ -508,6 +531,8 @@
     recv,
     box_send,
     box_recv,
+    near_send,
+    near_recv,
     sum_send,
     sum_recv,
     slots,
@@ -525,18 +550,21 @@
         load.start()
     groups = lax.axis_size("gz")
     barrier = pltpu.get_barrier_semaphore()
-    partners = 0
-    for axis in ("gz", "gy", "gx"):
-        for step in range(1, lax.axis_size(axis)):
-            pl.semaphore_signal(barrier, inc=1, device_id=place(axis, step), device_id_type=MESH)
-            partners += 1
+    partners = [place(axis, step) for axis in ("gx", "gz") for step in range(2, lax.axis_size(axis) - 1)]
+    partners += [place("gy", step) for step in range(2, lax.axis_size("gy") - 1)]
+    partners += [spot(*offset) for offset in ENDS + NEAR]
+    for partner in partners:
+        pl.semaphore_signal(barrier, inc=1, device_id=partner, device_id_type=MESH)
 
     for load in loads:
         load.wait()
     fine_bufs = (edge, packed, z0_in, y0_out, y0_in, yp0_in, xp0_in)
+    middle_bufs, low_bufs = (edge1, main1_in, edge1_in), (tiles2,)
     pack_boxes(slots, ids, stage, boxes, outgoing)
-
-    pl.semaphore_wait(barrier, partners)
+    mid = coarsen(kap0[4:20, 0:16, 0:LANES], shelf_c)
+    low = coarsen(mid, shelf_c)
+
+    pl.semaphore_wait(barrier, len(partners))
 
     ex_k0 = Fine(kap0, fine_bufs, 0, send, recv, 0)
     ex_k0.z_start()
@@ -557,27 +585,16 @@
         moves.append(copy)
     incoming[pl.ds(SEND * me, SEND)] = outgoing[pl.ds(SEND * me, SEND)]
 
-    mid = coarsen(kap0[4:20, 0:16, 0:LANES], shelf_c)
-    kap1[6:14, 0:8, :] = mid
-    kap2[4:8, 0:8, :] = coarsen(mid, shelf_c)
-    ex_k1 = Middle(kap1, z1_in.at[0], send, recv, 30)
-    ex_k2 = Low(kap2, z2_in.at[0], y2_in.at[0], send, recv, 36)
     ex_k0.z_finish(True)
     ex_k0.y_start()
-    ex_k1.z_start()
-    ex_k2.z_start()
     ex_k0.y_finish(True)
     ex_k0.x_start()
-    ex_k1.z_finish(True)
-    ex_k1.y_start()
-    ex_k2.z_finish(True)
-    ex_k2.y_start()
+    ex_k1 = Middle(kap1, middle_bufs, 0, near_send, near_recv, 0)
+    ex_k2 = Low(kap2, low_bufs, 0, near_send, near_recv, 26)
+    ex_k1.start(mid)
+    ex_k2.start(low)
     ex_k0.x_finish(True)
     make_stencil(kap0, sc0, dia0, inv0)
-    ex_k1.y_finish(True)
-    ex_k1.x_start()
-    ex_k2.y_finish(True)
-    ex_k2.x_start()
 
     for copy in moves:
         copy.wait()
@@ -586,13 +603,13 @@
     g0[4:20, 0:16, 0:LANES] = source[...] * inv0[4:20, 0:16, 0:LANES]
     ex_g0 = Fine(g0, fine_bufs, 1, send, recv, 10)
     ex_g0.z_start()
-    ex_k1.x_finish(True)
-    ex_k2.x_finish(True)
     ex_g0.z_finish(False)
     ex_g0.y_start()
+    ex_k1.finish(True)
     make_stencil(kap1, sc1, dia1, inv1)
     ex_g0.y_finish(False)
     ex_g0.x_start()
+    ex_k2.finish(True)
     make_stencil(kap2, sc2, dia2, inv2)
     ex_g0.x_finish(False)
     first_red(u0, g0, kap0)
@@ -608,40 +625,27 @@
 
     in_pieces(4, 20, 4, residual)
 
-    g1[6:14, 0:8, :] = 4.0 * coarsen(source[...], shelf_c) * inv1[6:14, 0:8, :]
-    ex_g1 = Middle(g1, z1_in.at[1], send, recv, 42)
+    ex_g1 = Middle(g1, middle_bufs, 1, near_send, near_recv, 52)
     ex_w0 = Fine(w0, fine_bufs, 2, send, recv, 20)
-    ex_g1.z_start()
-    ex_g1.z_finish(False)
-    ex_g1.y_start()
-    ex_g1.y_finish(False)
-    ex_g1.x_start()
+    ex_g1.start(4.0 * coarsen(source[...], shelf_c) * inv1[6:14, 0:8, :])
     ex_w0.z_start()
-    ex_g1.x_finish(False)
+    ex_g1.finish(False)
+    ex_w0.z_finish(False)
+    ex_w0.y_start()
     first_red(u1, g1, kap1)
     half_sweep(sc1, 1, 19, 1, ((u1, g1),), 6)
     half_sweep(sc1, 2, 18, 0, ((u1, g1),), 8)
     half_sweep(sc1, 3, 17, 1, ((u1, g1),), 14)
-    w1[6:14, 0:8, :] = u1[6:14, 0:8, :]
 
     here, total = around_sum(sc1, u1, 6, 8)
     rest = (0.25 * dia1[6:14]) * (g1[6:14] + total - here)
-    f2[4:8, 0:8, :] = coarsen(rest[:, 0:8], shelf_c)
-    ex_f2 = Low(f2, z2_in.at[1], y2_in.at[1], send, recv, 48)
-    ex_w1 = Middle(w1, z1_in.at[2], send, recv, 54)
-    ex_f2.z_start()
-    ex_w1.z_start()
-    ex_f2.z_finish(False)
-    ex_f2.y_start()
-    ex_w0.z_finish(False)
-    ex_w0.y_start()
-    ex_w1.z_finish(False)
-    ex_w1.y_start()
-    ex_f2.y_finish(False)
-    ex_f2.x_start()
+    ex_f2 = Low(f2, low_bufs, 1, near_send, near_recv, 78)
+    ex_w1 = Middle(w1, middle_bufs, 2, near_send, near_recv, 104)
+    ex_f2.start(coarsen(rest[:, 0:8], shelf_c))
+    ex_w1.start(jnp.where(iota((8, 8, LANES), 2) < 64, u1[6:14, 0:8, :], 0.0))
     ex_w0.y_finish(False)
     ex_w0.x_start()
-    ex_f2.x_finish(False)
+    ex_f2.finish(False)
     p2[...] = jnp.where(kap2[...] > 0.0, f2[...], 0.0)
 
     v2[0] = jnp.zeros((16, LANES), F32)
@@ -672,13 +676,11 @@
         "gx", sum_out.at[2], sum_x, sum_send, sum_recv, lax.axis_size("gy") + groups
     )
     sum_gy.start(tile)
-    ex_w1.y_finish(False)
-    ex_w1.x_start()
 
     refine_low(p2[...], shelf_r1, b1)
     refine_low(v2[...], shelf_r1, c1)
-    ex_w1.x_finish(False)
     sum_gz.start(sum_gy.finish())
+    ex_w1.finish(False)
     u1[...] = jnp.where(kap1[...] > 0.0, w1[...], 0.0)
     triple = ((u1, g1), (b1, None), (c1, None))
     half_sweep(sc1, 1, 19, 0, triple, 6)
@@ -768,9 +770,10 @@
             (3, 2, 8, 8, LANES),
             (3, 2, 8, LANES),
             (3, 2, 24, LANES),
-            (3, 2, 8, 8, LANES),
-            (2, 2, 4, 8, LANES),
-            (2, 2, 4, 8, LANES),
+            (3, 8, LANES),
+            (3, 9, 4, 8, LANES),
+            (3, 2, 9, 8, LANES),
+            (2, 3, 9, 8, LANES),
             (3, 8, LANES),
             (sizes["gy"], 8, LANES),
             (sizes["gz"], 8, LANES),
@@ -781,7 +784,7 @@
             for shape in shapes
         ]
         dma = pltpu.SemaphoreType.DMA
-        scratch += [dma((60,)), dma((60,)), dma((groups,)), dma((groups,))]
+        scratch += [dma((30,)), dma((30,)), dma((groups,)), dma((groups,)), dma((130,)), dma((130,))]
         scratch += [dma((sums,)), dma((sums,))]
         scratch += [pltpu.VMEM(old_slots.shape, jnp.bfloat16), pltpu.SMEM(old_ids.shape, jnp.int32)]
         scratch += [pltpu.SMEM(old_owner.shape, jnp.int32), dma((4,))]

time: 84.1 us -> 76.7 us (0.912)
  Pallas kernels: 82.3 us -> 75 us
    pallas_call x1, Pallas kernels: 82.3 us -> 75 us  [per_device(): pl.pallas_call(kernel, out_shape=jax.ShapeDtypeStruct(coefficient.shape,...]
where the time goes in v3:
time: 76.7 us; the launch traced here: 76.5 us
  Pallas kernels  75 us (98%)
  local copies, waits for them, and re-layouts  1.57 us (2%)
    pallas_call x1, Pallas kernels, per_device(): pl.pallas_call(kernel, out_shape=jax.ShapeDtypeStruct(coefficient.shape,...  75 us
    unnamed x1, local copies, waits for them, and re-layouts  1.57 us

profile of v3, /device:TPU:1, one launch (start us, length us, event | category | flops | bytes accessed | tf_op | source)
XLA Modules:
  0.0 76.5 jit_solution(14976577871884887432)
XLA Ops:
  0.0 75.0 %shard_map.46 = f32[16,16,128]{2,1,0:T(8,128)} custom-call(bf16[1,1,16,4096]{3,2,1,0:T(8,128)(2,1)} %slots_in.1, s32[1,1,16]{2,1,0:T(1,128)} %ids_in.1, s32[1,1,128]{2,1,0:T(1,128)} %owner_in.1, f32[16,16,128]{2,1,0:T(8,128)} %coefficient.1), custom_call_target="tpu_custom_call" | custom-call | tf_op jit(solution)/shard_map/pallas_call | solution.py:791
  75.0 1.6 %copy.6 = f32[16,16,128]{2,1,0:T(8,128)} copy(f32[16,16,128]{2,1,0:T(8,128)} %shard_map.46) | data formatting | bytes 262144

commit v4 on v3

--- a/solution.py
+++ b/solution.py
@@ -10,6 +10,7 @@
 BOX = 16
 NB = 8
 SEND = 2
+RELAY = -1
 LANES = 128
 MESH = pl.DeviceIdType.MESH
 F32 = jnp.float32
@@ -172,96 +173,72 @@
                     self.array[4 + 4 * dx + x, row : row + 8, :] = jnp.where(lane < 32, own, halo)
 
 
-class Fine:
+class Fine(Direct):
     def __init__(self, array, bufs, at, send, recv, base):
-        self.sems = [(send.at[base + i], recv.at[base + i]) for i in range(10)]
-        self.array, self.main = array, array.at[:, :, pl.ds(0, LANES)]
-        names = ("edge", "packed", "z_in", "y_out", "y_in", "yp_in", "xp_in")
-        for name, buf in zip(names, bufs):
-            setattr(self, name, buf.at[at])
-        self.all = {}
-
-    def pair(self, at, axis, up_src, up_dst, down_src, down_dst):
-        flying = [
-            remote(up_src, up_dst, *self.sems[at], axis, 1),
-            remote(down_src, down_dst, *self.sems[at + 1], axis, -1),
-        ]
-        for copy in flying:
-            copy.start()
-        self.all[at] = flying
-
-    def land(self, at):
-        for copy in self.all.pop(at):
-            copy.wait()
-
-    def z_start(self):
+        self.array, self.where = array, (send, recv, base)
+        self.edge, self.edge_in, self.y_out, self.y_in, self.corner_in = (buf.at[at] for buf in bufs)
+
+    def start(self):
         lane, sub = iota((16, LANES), 1), iota((8, LANES), 0)
         edge = jnp.zeros((16, LANES), F32)
         for x in range(16):
             rolled = pltpu.roll(self.array[4 + x, 0:16, 0:LANES], (8 * x + 4) % LANES, 1)
             edge = jnp.where(lane // 8 == x, rolled, edge)
         self.edge[...] = edge
-        self.pair(0, "gz", self.edge, self.z_in.at[0], self.edge, self.z_in.at[1])
         for x in range(8):
             near, far = self.array[4 + x, 8:16, 0:LANES], self.array[12 + x, 8:16, 0:LANES]
             self.y_out[0, x] = jnp.where(sub < 4, pltpu.roll(far, 4, 0), near)
             near, far = self.array[4 + x, 0:8, 0:LANES], self.array[12 + x, 0:8, 0:LANES]
             self.y_out[1, x] = jnp.where(sub < 4, near, pltpu.roll(far, 4, 0))
-        self.pair(2, "gy", self.y_out.at[0], self.y_in.at[0], self.y_out.at[1], self.y_in.at[1])
-
-    def z_finish(self, mask):
-        self.land(0)
-        lower, upper = self.z_in[0], self.z_in[1]
-        if mask:
-            lower, upper = lower * edge_scale("gz", -1), upper * edge_scale("gz", 1)
-        self.packed[0:16, :] = jnp.where(iota((16, LANES), 1) % 8 < 4, lower, upper)
-
-    def y_start(self):
-        high, low = self.packed.at[pl.ds(8, 8)], self.packed.at[pl.ds(0, 8)]
-        self.pair(4, "gy", high, self.yp_in.at[0], low, self.yp_in.at[1])
-
-    def y_finish(self, mask):
-        self.land(2)
+        plan = []
+        for dx, dy, dz in ENDS:
+            rows = {0: pl.ds(0, 16), 1: pl.ds(8, 8), -1: pl.ds(0, 8)}[dy]
+            into = self.edge_in.at[(1 - dz) // 2, block(-dx, -dy)]
+            plan.append(((dx, dy, dz), self.edge.at[rows], into.at[rows]))
+        inside = self.array.at[:, pl.ds(0, 16), pl.ds(0, LANES)]
+        for dx, dy, dz in NEAR:
+            if dy == 0:
+                src = inside.at[pl.ds(16 if dx > 0 else 4, 4)]
+                dst = inside.at[pl.ds(0 if dx > 0 else 20, 4)]
+            elif dx == 0:
+                src, dst = self.y_out.at[(1 - dy) // 2], self.y_in.at[(1 - dy) // 2]
+            else:
+                src = self.y_out.at[(1 - dy) // 2, pl.ds(4 if dx > 0 else 0, 4)]
+                dst = self.corner_in.at[(1 - dx) // 2, (1 - dy) // 2]
+            plan.append(((dx, dy, dz), src, dst))
+        self.begin(*self.where, plan)
+
+    def finish(self, mask):
+        self.land()
+        scales = scales_of(mask)
         low = iota((8, LANES), 0) < 4
-        scales = (edge_scale("gy", -1), edge_scale("gy", 1)) if mask else (1.0, 1.0)
         for x in range(8):
-            lower, upper = self.y_in[0, x], self.y_in[1, x]
-            if mask:
-                lower, upper = lower * scales[0], upper * scales[1]
+            lower = scaled_by(self.y_in[0, x], scales, 0, -1, 0)
+            upper = scaled_by(self.y_in[1, x], scales, 0, 1, 0)
             self.array[4 + x, 16:24, 0:LANES] = jnp.where(low, upper, lower)
             self.array[12 + x, 16:24, 0:LANES] = pltpu.roll(jnp.where(low, lower, upper), 4, 0)
-        main = self.main
-        self.pair(
-            6,
-            "gx",
-            main.at[pl.ds(16, 4)],
-            main.at[pl.ds(0, 4)],
-            main.at[pl.ds(4, 4)],
-            main.at[pl.ds(20, 4)],
-        )
-        self.land(4)
-        lower, upper = self.yp_in[0], self.yp_in[1]
+        for x in range(4):
+            lower = scaled_by(self.corner_in[0, 0, x], scales, -1, -1, 0)
+            upper = scaled_by(self.corner_in[0, 1, x], scales, -1, 1, 0)
+            self.array[x, 16:24, 0:LANES] = pltpu.roll(jnp.where(low, lower, upper), 4, 0)
+            lower = scaled_by(self.corner_in[1, 0, x], scales, 1, -1, 0)
+            upper = scaled_by(self.corner_in[1, 1, x], scales, 1, 1, 0)
+            self.array[20 + x, 16:24, 0:LANES] = jnp.where(low, upper, lower)
         if mask:
-            lower, upper = lower * scales[0], upper * scales[1]
-        self.packed[16:24, :] = jnp.where(low, upper, lower)
-
-    def x_start(self):
-        self.pair(8, "gx", self.packed, self.xp_in.at[0], self.packed, self.xp_in.at[1])
-        for x in range(16):
-            self.array[4 + x, :, LANES:] = pltpu.roll(self.packed[...], (256 - 8 * x - 4) % 128, 1)
-
-    def x_finish(self, mask):
-        self.land(8)
-        for x in range(4):
-            lower = pltpu.roll(self.xp_in[0], (256 - 8 * (12 + x) - 4) % LANES, 1)
-            upper = pltpu.roll(self.xp_in[1], (256 - 8 * x - 4) % LANES, 1)
-            if mask:
-                lower, upper = lower * edge_scale("gx", -1), upper * edge_scale("gx", 1)
-            self.array[x, :, LANES:], self.array[20 + x, :, LANES:] = lower, upper
-        self.land(6)
-        if mask:
-            self.array[0:4, :, 0:LANES] = self.array[0:4, :, 0:LANES] * edge_scale("gx", -1)
-            self.array[20:24, :, 0:LANES] = self.array[20:24, :, 0:LANES] * edge_scale("gx", 1)
+            for dx, first in ((-1, 0), (1, 20)):
+                face = self.array[first : first + 4, 0:16, 0:LANES]
+                self.array[first : first + 4, 0:16, 0:LANES] = scaled_by(face, scales, dx, 0, 0)
+        for dx, planes, first in ((-1, range(12, 16), 0), (0, range(16), 4), (1, range(4), 20)):
+            parts = []
+            for dy, rows in ((0, slice(0, 16)), (1, slice(0, 8)), (-1, slice(8, 16))):
+                lower = scaled_by(self.edge_in[0, block(dx, dy), rows], scales, dx, dy, -1)
+                upper = scaled_by(self.edge_in[1, block(dx, dy), rows], scales, dx, dy, 1)
+                parts.append(jnp.where(iota(lower.shape, 1) % 8 < 4, lower, upper))
+            body, tail = parts[0], jnp.where(low, parts[1], parts[2])
+            for at, x in enumerate(planes):
+                shift = (2 * LANES - 8 * x - 4) % LANES
+                self.array[first + at, 0:16, LANES:] = pltpu.roll(body, shift, 1)
+                self.array[first + at, 16:24, LANES:] = pltpu.roll(tail, shift, 1)
 
 
 def in_pieces(low, high, size, piece):
@@ -342,6 +319,19 @@
             values[x + at] = jnp.where(parity == at % 2, kept, 0.0)
 
     in_pieces(0, planes, 4, piece)
+
+
+def first_red_scaled(values, source, inverse, factor):
+    planes, rows, lanes = values.shape
+    parity = (iota((rows, lanes), 0) + iota((rows, lanes), 1)) % 2
+
+    def piece(x, count):
+        for at in range(count):
+            kept = factor * source[x + at] * inverse[x + at]
+            source[x + at] = kept
+            values[x + at] = jnp.where(parity == (1 + at) % 2, kept, 0.0)
+
+    in_pieces(1, planes - 1, 6, piece)
 
 
 def pair_matrix():
@@ -512,13 +502,11 @@
     shelf_r1,
     narrow,
     shelf_r0,
-    edge,
-    packed,
-    z0_in,
+    edge0,
+    edge0_in,
     y0_out,
     y0_in,
-    yp0_in,
-    xp0_in,
+    corner0_in,
     edge1,
     main1_in,
     edge1_in,
@@ -527,8 +515,6 @@
     sum_y,
     sum_z,
     sum_x,
-    send,
-    recv,
     box_send,
     box_recv,
     near_send,
@@ -539,6 +525,8 @@
     ids,
     owner,
     load_sem,
+    passing,
+    relay_sem,
 ):
     loads = [
         pltpu.make_async_copy(coefficient, kap0.at[pl.ds(4, 16), pl.ds(0, 16), pl.ds(0, LANES)], load_sem.at[0]),
@@ -558,7 +546,7 @@
 
     for load in loads:
         load.wait()
-    fine_bufs = (edge, packed, z0_in, y0_out, y0_in, yp0_in, xp0_in)
+    fine_bufs = (edge0, edge0_in, y0_out, y0_in, corner0_in)
     middle_bufs, low_bufs = (edge1, main1_in, edge1_in), (tiles2,)
     pack_boxes(slots, ids, stage, boxes, outgoing)
     mid = coarsen(kap0[4:20, 0:16, 0:LANES], shelf_c)
@@ -566,15 +554,22 @@
 
     pl.semaphore_wait(barrier, len(partners))
 
-    ex_k0 = Fine(kap0, fine_bufs, 0, send, recv, 0)
-    ex_k0.z_start()
+    ex_k0 = Fine(kap0, fine_bufs, 0, near_send, near_recv, 130)
+    ex_k0.start()
 
     me = lax.axis_index("gz")
     moves = []
-    for step in range(1, groups):
-        there = place("gz", step)["gz"]
+    relay = None
+    for step in sorted(range(1, groups), key=lambda step: -min(step, groups - step)):
+        boxes_there = outgoing.at[pl.ds(SEND * place("gz", step)["gz"], SEND)]
+        if RELAY and step == groups // 2:
+            relay = remote(
+                boxes_there, passing, relay_sem.at[0], relay_sem.at[1], "gz", RELAY * groups // 4
+            )
+            relay.start()
+            continue
         copy = remote(
-            outgoing.at[pl.ds(SEND * there, SEND)],
+            boxes_there,
             incoming.at[pl.ds(SEND * me, SEND)],
             box_send.at[step],
             box_recv.at[step],
@@ -585,15 +580,24 @@
         moves.append(copy)
     incoming[pl.ds(SEND * me, SEND)] = outgoing[pl.ds(SEND * me, SEND)]
 
-    ex_k0.z_finish(True)
-    ex_k0.y_start()
-    ex_k0.y_finish(True)
-    ex_k0.x_start()
+    ex_k0.finish(True)
+    if relay is not None:
+        relay.wait()
+        origin = place("gz", -RELAY * groups // 4)["gz"]
+        copy = remote(
+            passing,
+            incoming.at[pl.ds(SEND * origin, SEND)],
+            box_send.at[groups // 2],
+            box_recv.at[groups // 2],
+            "gz",
+            RELAY * groups // 4,
+        )
+        copy.start()
+        moves.append(copy)
     ex_k1 = Middle(kap1, middle_bufs, 0, near_send, near_recv, 0)
     ex_k2 = Low(kap2, low_bufs, 0, near_send, near_recv, 26)
     ex_k1.start(mid)
     ex_k2.start(low)
-    ex_k0.x_finish(True)
     make_stencil(kap0, sc0, dia0, inv0)
 
     for copy in moves:
@@ -601,17 +605,9 @@
     unpack_boxes(incoming, owner, box_shelf, source)
 
     g0[4:20, 0:16, 0:LANES] = source[...] * inv0[4:20, 0:16, 0:LANES]
-    ex_g0 = Fine(g0, fine_bufs, 1, send, recv, 10)
-    ex_g0.z_start()
-    ex_g0.z_finish(False)
-    ex_g0.y_start()
-    ex_k1.finish(True)
-    make_stencil(kap1, sc1, dia1, inv1)
-    ex_g0.y_finish(False)
-    ex_g0.x_start()
-    ex_k2.finish(True)
-    make_stencil(kap2, sc2, dia2, inv2)
-    ex_g0.x_finish(False)
+    ex_g0 = Fine(g0, fine_bufs, 1, near_send, near_recv, 156)
+    ex_g0.start()
+    ex_g0.finish(False)
     first_red(u0, g0, kap0)
     half_sweep(sc0, 1, 23, 1, ((u0, g0),), 4)
     half_sweep(sc0, 2, 22, 0, ((u0, g0),), 4)
@@ -626,16 +622,18 @@
     in_pieces(4, 20, 4, residual)
 
     ex_g1 = Middle(g1, middle_bufs, 1, near_send, near_recv, 52)
-    ex_w0 = Fine(w0, fine_bufs, 2, send, recv, 20)
-    ex_g1.start(4.0 * coarsen(source[...], shelf_c) * inv1[6:14, 0:8, :])
-    ex_w0.z_start()
+    ex_w0 = Fine(w0, fine_bufs, 2, near_send, near_recv, 182)
+    ex_g1.start(coarsen(source[...], shelf_c))
+    ex_k1.finish(True)
+    make_stencil(kap1, sc1, dia1, inv1)
+    ex_k2.finish(True)
+    make_stencil(kap2, sc2, dia2, inv2)
+    ex_w0.start()
     ex_g1.finish(False)
-    ex_w0.z_finish(False)
-    ex_w0.y_start()
-    first_red(u1, g1, kap1)
-    half_sweep(sc1, 1, 19, 1, ((u1, g1),), 6)
-    half_sweep(sc1, 2, 18, 0, ((u1, g1),), 8)
+    first_red_scaled(u1, g1, inv1, 4.0)
     half_sweep(sc1, 3, 17, 1, ((u1, g1),), 14)
+    half_sweep(sc1, 4, 16, 0, ((u1, g1),), 6)
+    half_sweep(sc1, 5, 15, 1, ((u1, g1),), 10)
 
     here, total = around_sum(sc1, u1, 6, 8)
     rest = (0.25 * dia1[6:14]) * (g1[6:14] + total - here)
@@ -643,8 +641,6 @@
     ex_w1 = Middle(w1, middle_bufs, 2, near_send, near_recv, 104)
     ex_f2.start(coarsen(rest[:, 0:8], shelf_c))
     ex_w1.start(jnp.where(iota((8, 8, LANES), 2) < 64, u1[6:14, 0:8, :], 0.0))
-    ex_w0.y_finish(False)
-    ex_w0.x_start()
     ex_f2.finish(False)
     p2[...] = jnp.where(kap2[...] > 0.0, f2[...], 0.0)
 
@@ -688,7 +684,7 @@
     half_sweep(sc1, 3, 17, 0, triple, 14)
     half_sweep(sc1, 4, 16, 1, triple, 6)
 
-    ex_w0.x_finish(False)
+    ex_w0.finish(False)
     refine_middle(u1, narrow, shelf_r0, u0, w0, kap0)
     sum_gx.start(sum_gz.finish())
     refine_middle(b1, narrow, shelf_r0, b0, None, None)
@@ -764,12 +760,10 @@
             (12, 16, LANES),
             (2, 12, 24, LANES),
             (3, 16, LANES),
-            (3, 24, LANES),
-            (3, 2, 16, LANES),
+            (3, 2, 9, 16, LANES),
             (3, 2, 8, 8, LANES),
             (3, 2, 8, 8, LANES),
-            (3, 2, 8, LANES),
-            (3, 2, 24, LANES),
+            (3, 2, 2, 4, 8, LANES),
             (3, 8, LANES),
             (3, 9, 4, 8, LANES),
             (3, 2, 9, 8, LANES),
@@ -784,10 +778,11 @@
             for shape in shapes
         ]
         dma = pltpu.SemaphoreType.DMA
-        scratch += [dma((30,)), dma((30,)), dma((groups,)), dma((groups,)), dma((130,)), dma((130,))]
+        scratch += [dma((groups,)), dma((groups,)), dma((208,)), dma((208,))]
         scratch += [dma((sums,)), dma((sums,))]
         scratch += [pltpu.VMEM(old_slots.shape, jnp.bfloat16), pltpu.SMEM(old_ids.shape, jnp.int32)]
         scratch += [pltpu.SMEM(old_owner.shape, jnp.int32), dma((4,))]
+        scratch += [pltpu.VMEM((SEND, 32, LANES), jnp.bfloat16), dma((2,))]
         return pl.pallas_call(
             kernel,
             out_shape=jax.ShapeDtypeStruct(coefficient.shape, F32),

time: 76.7 us -> 70.9 us (0.924)
  Pallas kernels: 75 us -> 69.1 us
    pallas_call x1, Pallas kernels: 75 us -> 69.1 us  [per_device(): pl.pallas_call(kernel, out_shape=jax.ShapeDtypeStruct(coefficient.shape,...]
where the time goes in v4:
time: 70.9 us; the launch traced here: 70.7 us
  Pallas kernels  69.1 us (97%)
  local copies, waits for them, and re-layouts  1.57 us (2%)
    pallas_call x1, Pallas kernels, per_device(): pl.pallas_call(kernel, out_shape=jax.ShapeDtypeStruct(coefficient.shape,...  69.1 us
    unnamed x1, local copies, waits for them, and re-layouts  1.57 us

profile of v4, /device:TPU:1, one launch (start us, length us, event | category | flops | bytes accessed | tf_op | source)
XLA Modules:
  0.0 70.7 jit_solution(16079798909346747011)
XLA Ops:
  0.0 69.1 %shard_map.46 = f32[16,16,128]{2,1,0:T(8,128)} custom-call(bf16[1,1,16,4096]{3,2,1,0:T(8,128)(2,1)} %slots_in.1, s32[1,1,16]{2,1,0:T(1,128)} %ids_in.1, s32[1,1,128]{2,1,0:T(1,128)} %owner_in.1, f32[16,16,128]{2,1,0:T(8,128)} %coefficient.1), custom_call_target="tpu_custom_call" | custom-call | tf_op jit(solution)/shard_map/pallas_call | solution.py:786
  69.2 1.6 %copy.6 = f32[16,16,128]{2,1,0:T(8,128)} copy(f32[16,16,128]{2,1,0:T(8,128)} %shard_map.46) | data formatting | bytes 262144

commit v5 on v4

--- a/solution.py
+++ b/solution.py
@@ -609,9 +609,9 @@
     ex_g0.start()
     ex_g0.finish(False)
     first_red(u0, g0, kap0)
-    half_sweep(sc0, 1, 23, 1, ((u0, g0),), 4)
-    half_sweep(sc0, 2, 22, 0, ((u0, g0),), 4)
-    half_sweep(sc0, 3, 21, 1, ((u0, g0),), 4)
+    half_sweep(sc0, 1, 23, 1, ((u0, g0),), 6)
+    half_sweep(sc0, 2, 22, 0, ((u0, g0),), 6)
+    half_sweep(sc0, 3, 21, 1, ((u0, g0),), 6)
     w0[4:20, 0:16, 0:LANES] = u0[4:20, 0:16, 0:LANES]
 
     def residual(x, count):
@@ -619,7 +619,7 @@
         rest = dia0[pl.ds(x, count)] * (g0[pl.ds(x, count)] + total - here)
         source[pl.ds(x - 4, count)] = rest[:, 0:16, 0:LANES]
 
-    in_pieces(4, 20, 4, residual)
+    in_pieces(4, 20, 8, residual)
 
     ex_g1 = Middle(g1, middle_bufs, 1, near_send, near_recv, 52)
     ex_w0 = Fine(w0, fine_bufs, 2, near_send, near_recv, 182)
@@ -628,7 +628,6 @@
     make_stencil(kap1, sc1, dia1, inv1)
     ex_k2.finish(True)
     make_stencil(kap2, sc2, dia2, inv2)
-    ex_w0.start()
     ex_g1.finish(False)
     first_red_scaled(u1, g1, inv1, 4.0)
     half_sweep(sc1, 3, 17, 1, ((u1, g1),), 14)
@@ -641,6 +640,7 @@
     ex_w1 = Middle(w1, middle_bufs, 2, near_send, near_recv, 104)
     ex_f2.start(coarsen(rest[:, 0:8], shelf_c))
     ex_w1.start(jnp.where(iota((8, 8, LANES), 2) < 64, u1[6:14, 0:8, :], 0.0))
+    ex_w0.start()
     ex_f2.finish(False)
     p2[...] = jnp.where(kap2[...] > 0.0, f2[...], 0.0)
 

time: 70.9 us -> 70.6 us (level)
  no operation moved by 1% of the time
where the time goes in v5:
time: 70.6 us; the launch traced here: 70.4 us
  Pallas kernels  68.9 us (98%)
  local copies, waits for them, and re-layouts  1.57 us (2%)
    pallas_call x1, Pallas kernels, per_device(): pl.pallas_call(kernel, out_shape=jax.ShapeDtypeStruct(coefficient.shape,...  68.9 us
    unnamed x1, local copies, waits for them, and re-layouts  1.57 us

profile of v5, /device:TPU:1, one launch (start us, length us, event | category | flops | bytes accessed | tf_op | source)
XLA Modules:
  0.0 70.4 jit_solution(1085119153658456643)
XLA Ops:
  0.0 68.9 %shard_map.46 = f32[16,16,128]{2,1,0:T(8,128)} custom-call(bf16[1,1,16,4096]{3,2,1,0:T(8,128)(2,1)} %slots_in.1, s32[1,1,16]{2,1,0:T(1,128)} %ids_in.1, s32[1,1,128]{2,1,0:T(1,128)} %owner_in.1, f32[16,16,128]{2,1,0:T(8,128)} %coefficient.1), custom_call_target="tpu_custom_call" | custom-call | tf_op jit(solution)/shard_map/pallas_call | solution.py:786
  68.9 1.6 %copy.6 = f32[16,16,128]{2,1,0:T(8,128)} copy(f32[16,16,128]{2,1,0:T(8,128)} %shard_map.46) | data formatting | bytes 262144
